TPU v7x, 16 devices: a 4x2x1 block of a 4x4x8 slice. The times are simulated.
16 devices in a mesh: dp: 2 (over y, z), sp: 8 (over x, core).
Axes of the slice: x: 4, y: 2, z: 1, core: 2. Of those that a mesh axis runs over, the one named last changes fastest.
The devices are a block of a 4x4x8 slice.
Arguments:
- tokens: bfloat16 [32768, 512], P(('dp', 'sp')), parts along dimension 0
- grad_out: bfloat16 [32768, 512], P(('dp', 'sp')), parts along dimension 0
- ln_gain: float32 [512], replicated
- ln_bias: float32 [512], replicated
- w_qkv: bfloat16 [512, 1536], replicated
- w_out: bfloat16 [512, 512], replicated
- temperature: float32 [8], replicated
Outputs:
- output 1: bfloat16 [32768, 512], P(('dp', 'sp')), parts along dimension 0
- output 2: bfloat16 [32768, 512], P(('dp', 'sp')), parts along dimension 0
- output 3: float32 [1024, 1536], P(('dp', 'sp')), parts along dimension 0
- output 4: float32 [1024, 512], P(('dp', 'sp')), parts along dimension 0
- output 5: float32 [1024], P('dp'), parts along dimension 0
- output 6: float32 [1024], P('dp'), parts along dimension 0
- output 7: float32 [16], P('dp'), parts along dimension 0
There are 2 independent parts. A program takes and returns all parts, laid end to end along the dimension named above; an argument that names none is the same for every part.
All inputs are finite; a program needn't handle non-finite values.
Results may differ from a plain program's by a relative error of at most 0.00113883.
Values are sent between devices in bfloat16 or wider.
A program may use at most 768 MiB of HBM per device.

v0:
```python
import jax
import jax.numpy as jnp
from jax import lax
from jax.sharding import PartitionSpec as P


def layer_norm(x_f32, ln_gain, ln_bias):
    row_mean = jnp.mean(x_f32, axis=-1, keepdims=True)
    centered = x_f32 - row_mean
    row_var = jnp.mean(centered * centered, axis=-1, keepdims=True)
    return centered * lax.rsqrt(row_var + 1e-6) * ln_gain + ln_bias


def attn_probs(gram_sum, q_sq, k_sq, value_a11):
    cosine = gram_sum / (jnp.sqrt(q_sq)[..., :, None] * jnp.sqrt(k_sq)[..., None, :])
    return jax.nn.softmax(value_a11[..., None, None] * cosine, axis=-1)


def project(x_rows, ln_gain, ln_bias, w_qkv, num_heads):
    ln_value, ln_vjp = jax.vjp(layer_norm, x_rows.astype(jnp.float32), ln_gain, ln_bias)
    normed = ln_value.astype(jnp.bfloat16)
    qkv_act = jnp.dot(normed, w_qkv, preferred_element_type=jnp.float32).astype(jnp.bfloat16)
    qkv_heads = qkv_act.reshape(x_rows.shape[0], 3, num_heads, -1)
    return ln_vjp, normed, qkv_heads[:, 0], qkv_heads[:, 1], qkv_heads[:, 2]


def apply_attn(v_heads, attn_weights):
    attn_out = jnp.einsum('nhj,hij->nhi', v_heads, attn_weights, preferred_element_type=jnp.float32)
    return attn_out.astype(jnp.bfloat16).reshape(v_heads.shape[0], -1)


def solution(mesh):
    row_spec = P(('dp', 'sp'), None)
    part_spec = P('dp')
    full_spec = P()

    def local_step(x_loc, dy_loc, ln_gain, ln_bias, w_qkv, w_out, value_a11):
        local_rows, model_width = x_loc.shape
        num_heads = value_a11.shape[0]
        fwd_act = project(x_loc, ln_gain, ln_bias, w_qkv, num_heads)
        q_heads, k_heads, v_heads = fwd_act[2], fwd_act[3], fwd_act[4]
        gram_part = jnp.einsum('nhi,nhj->hij', q_heads, k_heads, preferred_element_type=jnp.float32)
        qsq_part = jnp.einsum('nhi,nhi->hi', q_heads, q_heads, preferred_element_type=jnp.float32)
        ksq_part = jnp.einsum('nhj,nhj->hj', k_heads, k_heads, preferred_element_type=jnp.float32)
        gram_sum, q_sq, k_sq = lax.psum((gram_part, qsq_part, ksq_part), 'sp')
        attn_weights = attn_probs(gram_sum, q_sq, k_sq, value_a11).astype(jnp.bfloat16)
        attn_out = apply_attn(v_heads, attn_weights)
        out_proj = jnp.dot(attn_out, w_out, preferred_element_type=jnp.float32)
        out_tokens = (x_loc.astype(jnp.float32) + out_proj).astype(jnp.bfloat16)

        x_again, gram_kept, qsq_kept, ksq_kept = lax.optimization_barrier((x_loc, gram_sum, q_sq, k_sq))
        ln_vjp, normed, q_heads, k_heads, v_heads = project(x_again, ln_gain, ln_bias, w_qkv, num_heads)
        attn_f32, probs_vjp = jax.vjp(attn_probs, gram_kept, qsq_kept, ksq_kept, value_a11)
        attn_weights = attn_f32.astype(jnp.bfloat16)
        attn_out = apply_attn(v_heads, attn_weights)
        wout_part = jnp.einsum('nc,nd->cd', attn_out, dy_loc, preferred_element_type=jnp.float32)
        grad_w_out = lax.psum_scatter(wout_part, 'sp', scatter_dimension=0, tiled=True)
        d_attn = jnp.einsum('nd,cd->nc', dy_loc, w_out, preferred_element_type=jnp.float32)
        d_attn = d_attn.astype(jnp.bfloat16).reshape(local_rows, num_heads, -1)
        probs_part = jnp.einsum('nhi,nhj->hij', d_attn, v_heads, preferred_element_type=jnp.float32)
        d_probs = lax.psum(probs_part, 'sp')
        d_gram, d_qsq, d_ksq, value_a16 = probs_vjp(d_probs)
        d_gram_bf = d_gram.astype(jnp.bfloat16)
        d_q = jnp.einsum('hij,nhj->nhi', d_gram_bf, k_heads, preferred_element_type=jnp.float32) + 2.0 * q_heads * d_qsq
        d_k = jnp.einsum('hij,nhi->nhj', d_gram_bf, q_heads, preferred_element_type=jnp.float32) + 2.0 * k_heads * d_ksq
        d_v = jnp.einsum('hij,nhi->nhj', attn_weights, d_attn, preferred_element_type=jnp.float32)
        d_qkv = jnp.stack([d_q, d_k, d_v], axis=1).astype(jnp.bfloat16).reshape(local_rows, 3 * model_width)
        wqkv_part = jnp.einsum('nc,nk->ck', normed, d_qkv, preferred_element_type=jnp.float32)
        grad_w_qkv = lax.psum_scatter(wqkv_part, 'sp', scatter_dimension=0, tiled=True)
        d_normed = jnp.einsum('nk,ck->nc', d_qkv, w_qkv, preferred_element_type=jnp.float32)
        d_x, gain_part, bias_part = ln_vjp(d_normed)
        grad_gain, grad_bias = lax.psum((gain_part, bias_part), 'sp')
        grad_tokens = (dy_loc.astype(jnp.float32) + d_x).astype(jnp.bfloat16)
        return out_tokens, grad_tokens, grad_w_qkv, grad_w_out, grad_gain, grad_bias, value_a16

    return jax.shard_map(local_step, mesh=mesh,
                         in_specs=(row_spec, row_spec, full_spec, full_spec, full_spec, full_spec, full_spec),
                         out_specs=(row_spec, row_spec, row_spec, row_spec, part_spec, part_spec, part_spec),
                         check_vma=False)
```

profile of v0, /device:TPU:112, one launch (start us, length us, event | category | flops | bytes accessed | tf_op | source)
XLA Modules:
  0.0 217.9 jit_solution(641038671826796468)
XLA Ops:
  7.2 0.0 copy-start
  7.2 0.0 copy-start.12
  7.2 0.0 copy-start.14
  7.2 0.1 all-reduce.5.cloned.1.call-start
  7.3 0.0 copy-start.1
  7.3 2.1 convert_reduce_fusion
  9.4 2.5 %fusion.13 = f32[2048]{0:T(1024)S(1)} fusion(bf16[2048,512]{1,0:T(8,128)(2,1)} %param.7, f32[2048]{0:T(1024)S(1)} %broadcast_multiply_fusion.1), kind=kLoop, calls=%fused_computation.22 | loop fusion | flops 4192256 | bytes 2113536 | tf_op jit(solution)/shard_map/jvp()/reduce_sum | solution.py:10
  11.9 0.0 copy-done
  11.9 0.0 copy-done.12
  11.9 0.0 copy-done.14
  11.9 0.0 copy-done.1
  11.9 4.1 %convolution_convert_fusion.1 = bf16[2048,1536]{0,1:T(8,128)(2,1)S(1)} fusion(bf16[512,1536]{1,0:T(8,128)(2,1)S(1)} %copy-done, bf16[2048,512]{1,0:T(8,128)(2,1)S(1)} %copy-done.1, f32[512]{0:T(512)S(1)} %copy-done.14, f32[512]{0:T(512)S(1)} %copy-done.12, f32[2048]{0:T(1024)S(1)} %add_rsqrt_fusion, f32[2048]{0:T(1024)S(1)} %broadcast_multiply_fusion.1), kind=kOutput, calls=%fused_computation.3 | convolution fusion | flops 3230662656 | bytes 9981952 | tf_op jit(solution)/shard_map/dot_general | solution.py:22
  16.1 0.0 copy-start.7
  16.1 0.0 copy-start.13
  16.1 2.6 %copy-done.7 = bf16[2048,1536]{0,1:T(8,128)(2,1)} copy-done((bf16[2048,1536]{0,1:T(8,128)(2,1)}, bf16[2048,1536]{0,1:T(8,128)(2,1)S(1)}, u32[]{:S(2)}) %copy-start.7) | copy-done | bytes 6291480
  18.7 1.4 fusion.28
  20.1 0.1 all-reduce.5.cloned.1.call-update
  20.2 0.1 all-reduce.7.cloned.1.call-start
  20.3 0.0 copy-done.13
  20.3 0.0 copy-start.8
  20.3 4.3 %convolution_convert_fusion.4 = bf16[2048,512]{0,1:T(8,128)(2,1)} fusion(bf16[2048,512]{1,0:T(8,128)(2,1)} %param.8, bf16[512,512]{1,0:T(8,128)(2,1)S(1)} %copy-done.13), kind=kOutput, calls=%fused_computation.40 | convolution fusion | flops 1074790400 | bytes 4718592 | tf_op jit(solution)/shard_map/nd,cd->nc/dot_general | solution.py:58
  24.6 0.0 copy-done.8
  24.6 0.9 fusion.23
  25.5 16.1 %all-reduce.1 = (f32[8,64]{1,0:T(8,128)S(1)}, f32[8,64]{1,0:T(8,128)S(1)}) all-reduce(f32[8,64]{1,0:T(8,128)S(1)} %get-tuple-element.18, f32[8,64]{1,0:T(8,128)S(1)} %get-tuple-element.17), channel_id=1, replica_groups=mesh['dp'=2,'sp'=8] {'sp'}, use_global_device_ids=true, to_apply=%region_4.0 | all-reduce | flops 1024 | bytes 8192 | tf_op jit(solution)/shard_map/psum | solution.py:45
  41.6 33.8 %all-reduce.5.cloned.1.call-done = f32[8,64,64]{2,1,0:T(8,128)} async-done(((f32[8,64,64]{2,1,0:T(8,128)}), f32[8,64,64]{2,1,0:T(8,128)}) %all-reduce.5.cloned.1.call-update) | async-done | bytes 131088 | tf_op jit(solution)/shard_map/psum | solution.py:45
  75.4 2.1 convert_reduce_fusion.1
  77.5 2.5 %fusion.17 = f32[2048]{0:T(1024)S(1)} fusion(bf16[2048,512]{1,0:T(8,128)(2,1)} %param.7, f32[2048]{0:T(1024)S(1)} %broadcast_multiply_fusion), kind=kLoop, calls=%fused_computation.26 | loop fusion | flops 4192256 | bytes 2113536 | tf_op jit(solution)/shard_map/jvp()/reduce_sum | solution.py:10
  80.0 0.0 copy-done.11
  80.0 0.0 copy-done.10
  80.0 2.0 fusion.69
  82.1 0.0 copy-done.2
  82.1 5.8 %convolution_convert_fusion = bf16[2048,1536]{0,1:T(8,128)(2,1)} fusion(bf16[512,1536]{1,0:T(8,128)(2,1)S(1)} %copy-done, bf16[2048,512]{1,0:T(8,128)(2,1)S(1)} %copy-done.2, f32[2048]{0:T(1024)S(1)} %fusion.50, f32[2048]{0:T(1024)S(1)} %broadcast_multiply_fusion, f32[512]{0:T(512)S(1)} %copy-done.14, f32[512]{0:T(512)S(1)} %copy-done.12), kind=kOutput, calls=%fused_computation.2 | convolution fusion | flops 3230662656 | bytes 9981952 | tf_op jit(solution)/shard_map/dot_general | solution.py:22
  87.9 5.1 %convolution_convert_fusion.2 = bf16[8,64,2048]{2,1,0:T(8,128)(2,1)} fusion(bf16[2048,3,8,64]{0,3,2,1:T(8,128)(2,1)} %bitcast.85, f32[8,64]{1,0:T(8,128)S(1)} %get-tuple-element.30, f32[8]{0:T(128)S(1)} %copy-done.11, f32[8,64,64]{2,1,0:T(8,128)S(1)} %copy-done.10, f32[8,64]{1,0:T(8,128)S(1)} %sqrt.15, f32[8,64]{1,0:T(8,128)S(1)} %sqrt.14), kind=kOutput, calls=%fused_computation.38 | convolution fusion | flops 135463488 | bytes 4331552 | tf_op jit(solution)/shard_map/nhj,hij->nhi/dot_general | solution.py:28
  93.0 3.6 %fusion.35 = f32[8,64,64]{2,1,0:T(8,128)} fusion(bf16[2048,8,64]{0,2,1:T(8,128)(2,1)} %bitcast.81, bf16[2048,3,8,64]{0,3,2,1:T(8,128)(2,1)} %bitcast.86), kind=kOutput, calls=%fused_computation.56 | convolution fusion | flops 134217728 | bytes 4325376 | tf_op jit(solution)/shard_map/nhi,nhj->hij/dot_general | solution.py:60
  96.6 0.1 all-reduce.7.cloned.1.call-update
  96.6 0.2 reduce-scatter.5.cloned.1.call-start
  96.9 4.5 %fusion.70 = f32[512,512]{1,0:T(8,128)} fusion(bf16[2048,512]{0,1:T(8,128)(2,1)} %bitcast.83, bf16[2048,512]{1,0:T(8,128)(2,1)} %param.8), kind=kOutput, calls=%fused_computation.100 | convolution fusion | flops 1073741824 | bytes 5242880 | tf_op jit(solution)/shard_map/nc,nd->cd/dot_general | solution.py:56
  101.4 5.4 %fusion.26 = bf16[2048,1,8,64]{0,3,2,1:T(8,128)(2,1)} fusion(bf16[2048,8,64]{0,2,1:T(8,128)(2,1)} %bitcast.82, f32[8,64]{1,0:T(8,128)S(1)} %get-tuple-element.30, f32[8]{0:T(128)S(1)} %copy-done.11, f32[8,64,64]{2,1,0:T(8,128)S(1)} %copy-done.10, f32[8,64]{1,0:T(8,128)S(1)} %sqrt.15, f32[8,64]{1,0:T(8,128)S(1)} %sqrt.14), kind=kOutput, calls=%fused_computation.44 | convolution fusion | flops 135463488 | bytes 4331552 | tf_op jit(solution)/shard_map/hij,nhi->nhj/dot_general | solution.py:66
  106.7 0.1 reduce-scatter.5.cloned.1.call-update
  106.8 0.1 reduce-scatter.3.cloned.1.call-start
  106.9 40.9 %all-reduce.7.cloned.1.call-done = f32[8,64,64]{2,1,0:T(8,128)} async-done(((f32[8,64,64]{2,1,0:T(8,128)}), f32[8,64,64]{2,1,0:T(8,128)}) %all-reduce.7.cloned.1.call-update) | async-done | bytes 131088 | tf_op jit(solution)/shard_map/psum | solution.py:61
  147.8 1.2 multiply_reduce_fusion.3
  149.0 1.2 fusion.46
  150.3 0.8 multiply_reduce_fusion.2
  151.1 3.2 %fusion.24 = bf16[2048,1,8,64]{0,3,2,1:T(8,128)(2,1)S(1)} fusion(f32[8,64]{1,0:T(8,128)S(1)} %get-tuple-element.34, bf16[2048,3,8,64]{0,3,2,1:T(8,128)(2,1)} %bitcast.87, f32[8,64,64]{2,1,0:T(8,128)S(1)} %get-tuple-element.29, f32[8,64]{1,0:T(8,128)S(1)} %sqrt.15, f32[8,64]{1,0:T(8,128)S(1)} %sqrt.14, f32[8]{0:T(128)S(1)} %copy-done.11), kind=kOutput, calls=%fused_computation.42 | convolution fusion | flops 139591680 | bytes 6428704 | tf_op jit(solution)/shard_map/hij,nhj->nhi/dot_general | solution.py:64
  154.2 0.0 copy-start.6
  154.2 3.6 %fusion.25 = bf16[2048,1,8,64]{0,3,2,1:T(8,128)(2,1)S(1)} fusion(f32[8,64]{1,0:T(8,128)S(1)} %get-tuple-element.33, bf16[2048,3,8,64]{0,3,2,1:T(8,128)(2,1)} %bitcast.88, f32[8,64,64]{2,1,0:T(8,128)S(1)} %get-tuple-element.29, f32[8,64]{1,0:T(8,128)S(1)} %sqrt.15, f32[8,64]{1,0:T(8,128)S(1)} %sqrt.14, f32[8]{0:T(128)S(1)} %copy-done.11), kind=kOutput, calls=%fused_computation.43 | convolution fusion | flops 139591680 | bytes 6428704 | tf_op jit(solution)/shard_map/hij,nhi->nhj/dot_general | solution.py:65
  157.9 0.0 copy-done.6
  157.9 0.0 copy-start.3
  157.9 0.7 pad_maximum_fusion
  158.6 0.0 copy-start.9
  158.6 2.6 %copy-done.9 = bf16[2048,3,8,64]{0,3,2,1:T(8,128)(2,1)} copy-done((bf16[2048,3,8,64]{0,3,2,1:T(8,128)(2,1)}, bf16[2048,3,8,64]{0,3,2,1:T(8,128)(2,1)S(1)}, u32[]{:S(2)}) %copy-start.9) | copy-done | bytes 6291480
  161.2 6.0 %fusion.63 = f32[512,1536]{1,0:T(8,128)} fusion(bf16[2048,1536]{0,1:T(8,128)(2,1)S(1)} %bitcast.79, bf16[2048,512]{1,0:T(8,128)(2,1)S(1)} %copy-done.3, f32[2048]{0:T(1024)S(1)} %fusion.50, f32[2048]{0:T(1024)S(1)} %broadcast_multiply_fusion, f32[512]{0:T(512)S(1)} %copy-done.14, f32[512]{0:T(512)S(1)} %copy-done.12), kind=kOutput, calls=%fused_computation.95 | convolution fusion | flops 3227516928 | bytes 11554816 | tf_op jit(solution)/shard_map/nc,nk->ck/dot_general | solution.py:68
  167.2 0.1 reduce-scatter.3.cloned.1.call-update
  167.3 2.1 fusion.68
  169.4 5.1 %convolution_convert_fusion.5 = bf16[8,64,2048]{2,1,0:T(8,128)(2,1)} fusion(bf16[2048,3,8,64]{0,3,2,1:T(8,128)(2,1)} %bitcast.77, f32[8,64]{1,0:T(8,128)S(1)} %fusion.68, f32[8,64,64]{2,1,0:T(8,128)S(1)} %copy-done.10, f32[8,64]{1,0:T(8,128)S(1)} %sqrt.13, f32[8,64]{1,0:T(8,128)S(1)} %sqrt.12, f32[8]{0:T(128)S(1)} %copy-done.11), kind=kOutput, calls=%fused_computation.41 | convolution fusion | flops 135463488 | bytes 4331552 | tf_op jit(solution)/shard_map/nhj,hij->nhi/dot_general | solution.py:28
  174.5 5.0 %fusion.19 = bf16[2048,512]{1,0:T(8,128)(2,1)} fusion(bf16[2048,512]{1,0:T(8,128)(2,1)} %param.7, bf16[2048,512]{0,1:T(8,128)(2,1)} %bitcast.84, bf16[512,512]{1,0:T(8,128)(2,1)S(1)} %copy-done.13), kind=kOutput, calls=%fused_computation.28 | convolution fusion | flops 1076887552 | bytes 6815744 | tf_op jit(solution)/shard_map/dot_general | solution.py:48
  179.5 0.0 copy-done.4
  179.5 6.4 %fusion.67 = (f32[512]{0:T(512)S(1)}, f32[2048]{0:T(1024)S(1)}, f32[2048,512]{1,0:T(8,128)S(1)}) fusion(f32[512]{0:T(512)S(1)} %copy-done.12, f32[2048]{0:T(1024)S(1)} %broadcast_multiply_fusion, bf16[2048,512]{1,0:T(8,128)(2,1)S(1)} %copy-done.4, bf16[2048,1536]{0,1:T(8,128)(2,1)} %bitcast.80, bf16[512,1536]{1,0:T(8,128)(2,1)S(1)} %copy-done), kind=kOutput, calls=%fused_computation.97 | convolution fusion | flops 3227514368 | bytes 14176256 | tf_op jit(solution)/shard_map/nk,ck->nc/dot_general | solution.py:70
  186.0 2.1 fusion.12
  188.1 0.0 copy-done.5
  188.2 13.8 %all-reduce = (f32[512]{0:T(512)}, f32[512]{0:T(512)}) all-reduce(f32[512]{0:T(512)S(1)} %get-tuple-element.15, f32[512]{0:T(512)S(1)} %get-tuple-element.19), channel_id=1, replica_groups=mesh['dp'=2,'sp'=8] {'sp'}, use_global_device_ids=true, to_apply=%region_20.0 | all-reduce | flops 1024 | bytes 8192 | tf_op jit(solution)/shard_map/psum | solution.py:72
  202.0 5.3 %add_convert_fusion = bf16[2048,512]{1,0:T(8,128)(2,1)} fusion(bf16[2048,512]{1,0:T(8,128)(2,1)} %param.8, f32[2048]{0:T(1024)S(1)} %negate_multiply_fusion, f32[2048]{0:T(1024)S(1)} %multiply_multiply_fusion.1, f32[2048]{0:T(1024)S(1)} %broadcast_multiply_fusion, bf16[2048,512]{1,0:T(8,128)(2,1)} %param.7, f32[2048]{0:T(1024)S(1)} %fusion.50, ...), kind=kLoop, calls=%fused_computation.37 | loop fusion | flops 11534336 | bytes 10520576 | tf_op jit(solution)/shard_map/convert_element_type | solution.py:73
  207.3 4.1 %reduce-scatter.3.cloned.1.call-done = f32[64,1536]{1,0:T(8,128)} async-done(((f32[512,1536]{1,0:T(8,128)}), f32[64,1536]{1,0:T(8,128)}) %reduce-scatter.3.cloned.1.call-update) | async-done | bytes 393232 | tf_op jit(solution)/shard_map/reduce_scatter | solution.py:69
  (20 shorter events, 0.1 us)
Async XLA Ops:
  7.2 4.7 %copy-start = (bf16[512,1536]{1,0:T(8,128)(2,1)S(1)}, bf16[512,1536]{1,0:T(8,128)(2,1)}, u32[]{:S(2)}) copy-start(bf16[512,1536]{1,0:T(8,128)(2,1)} %param.11) | copy-start | bytes 4718596
  7.2 4.7 %copy-start.12 = (f32[512]{0:T(512)S(1)}, f32[512]{0:T(512)}, u32[]{:S(2)}) copy-start(f32[512]{0:T(512)} %param.9) | copy-start | bytes 6148
  7.2 4.7 %copy-start.14 = (f32[512]{0:T(512)S(1)}, f32[512]{0:T(512)}, u32[]{:S(2)}) copy-start(f32[512]{0:T(512)} %param.10) | copy-start | bytes 6148
  7.2 68.2 %all-reduce.5.cloned.1.call-start = ((), (), s32[]{:S(2)}) async-start(), calls=%async_computation.2 | async-start | bytes 524288 | tf_op jit(solution)/shard_map/psum | solution.py:45
  7.3 4.6 %copy-start.1 = (bf16[2048,512]{1,0:T(8,128)(2,1)S(1)}, bf16[2048,512]{1,0:T(8,128)(2,1)}, u32[]{:S(2)}) copy-start(bf16[2048,512]{1,0:T(8,128)(2,1)} %param.7) | copy-start | bytes 6291460
  16.1 2.7 %copy-start.7 = (bf16[2048,1536]{0,1:T(8,128)(2,1)}, bf16[2048,1536]{0,1:T(8,128)(2,1)S(1)}, u32[]{:S(2)}) copy-start(bf16[2048,1536]{0,1:T(8,128)(2,1)S(1)} %convolution_convert_fusion.1) | copy-start | bytes 18874372
  16.1 4.2 %copy-start.13 = (bf16[512,512]{1,0:T(8,128)(2,1)S(1)}, bf16[512,512]{1,0:T(8,128)(2,1)}, u32[]{:S(2)}) copy-start(bf16[512,512]{1,0:T(8,128)(2,1)} %param.12) | copy-start | bytes 1572868
  20.2 127.6 %all-reduce.7.cloned.1.call-start = ((), (), s32[]{:S(2)}) async-start(), calls=%async_computation.3 | async-start | bytes 524288 | tf_op jit(solution)/shard_map/psum | solution.py:61
  20.3 4.4 %copy-start.8 = (bf16[2048,1536]{0,1:T(8,128)(2,1)S(1)}, bf16[2048,1536]{0,1:T(8,128)(2,1)}, u32[]{:S(2)}) copy-start(bf16[2048,1536]{0,1:T(8,128)(2,1)} %copy-done.7) | copy-start | bytes 18874372
  24.6 55.4 %copy-start.11 = (f32[8]{0:T(128)S(1)}, f32[8]{0:T(128)}, u32[]{:S(2)}) copy-start(f32[8]{0:T(128)} %param.13) | copy-start | bytes 100
  75.4 4.6 %copy-start.10 = (f32[8,64,64]{2,1,0:T(8,128)S(1)}, f32[8,64,64]{2,1,0:T(8,128)}, u32[]{:S(2)}) copy-start(f32[8,64,64]{2,1,0:T(8,128)} %all-reduce.5.cloned.1.call-done) | copy-start | bytes 393220
  75.4 6.7 %copy-start.2 = (bf16[2048,512]{1,0:T(8,128)(2,1)S(1)}, bf16[2048,512]{1,0:T(8,128)(2,1)}, u32[]{:S(2)}) copy-start(bf16[2048,512]{1,0:T(8,128)(2,1)} %param.7) | copy-start | bytes 6291460
  96.6 110.6 %reduce-scatter.5.cloned.1.call-start = ((), (), s32[]{:S(2)}) async-start(), calls=%async_computation.5 | async-start | bytes 1179648 | tf_op jit(solution)/shard_map/reduce_scatter | solution.py:57
  106.8 104.5 %reduce-scatter.3.cloned.1.call-start = ((), (), s32[]{:S(2)}) async-start(), calls=%async_computation.4 | async-start | bytes 3538944 | tf_op jit(solution)/shard_map/reduce_scatter | solution.py:69
  154.2 3.6 %copy-start.6 = (bf16[2048,1,8,64]{0,3,2,1:T(8,128)(2,1)S(1)}, bf16[2048,1,8,64]{0,3,2,1:T(8,128)(2,1)}, u32[]{:S(2)}) copy-start(bf16[2048,1,8,64]{0,3,2,1:T(8,128)(2,1)} %fusion.26) | copy-start | bytes 6291460
  157.9 3.4 %copy-start.3 = (bf16[2048,512]{1,0:T(8,128)(2,1)S(1)}, bf16[2048,512]{1,0:T(8,128)(2,1)}, u32[]{:S(2)}) copy-start(bf16[2048,512]{1,0:T(8,128)(2,1)} %param.7) | copy-start | bytes 6291460
  158.6 2.7 %copy-start.9 = (bf16[2048,3,8,64]{0,3,2,1:T(8,128)(2,1)}, bf16[2048,3,8,64]{0,3,2,1:T(8,128)(2,1)S(1)}, u32[]{:S(2)}) copy-start(bf16[2048,3,8,64]{0,3,2,1:T(8,128)(2,1)S(1)} %pad_maximum_fusion) | copy-start | bytes 18874372
  174.5 5.0 %copy-start.4 = (bf16[2048,512]{1,0:T(8,128)(2,1)S(1)}, bf16[2048,512]{1,0:T(8,128)(2,1)}, u32[]{:S(2)}) copy-start(bf16[2048,512]{1,0:T(8,128)(2,1)} %param.7) | copy-start | bytes 6291460
  186.0 2.2 copy-start.5
Sparse Core Ops, SparseCore 0:
  20.3 55.0 all-reduce.4
  96.8 50.9 all-reduce.6
  150.6 27.1 reduce-scatter.4
  180.6 30.7 reduce-scatter.2
where the time goes:
time: 218 us
  waiting for transfers between devices  79 us (36%)
  matrix products  63.5 us (29%)
  blocking collectives  29.9 us (14%)
  other arithmetic  25.5 us (12%)
  between operations  14.1 us (6%)
  local copies, waits for them, and re-layouts  5.38 us (2%)
    psum x1, waiting for transfers between devices, local_step(): d_probs = lax.psum(probs_part, 'sp')  40.9 us
    psum x1, waiting for transfers between devices, local_step(): gram_sum, q_sq, k_sq = lax.psum((gram_part, qsq_part, ksq_part), 'sp')  33.8 us
    psum x1, blocking collectives, local_step(): gram_sum, q_sq, k_sq = lax.psum((gram_part, qsq_part, ksq_part), 'sp')  16.1 us
    psum x1, blocking collectives, local_step(): grad_gain, grad_bias = lax.psum((gain_part, bias_part), 'sp')  13.8 us
    dot_general x2, matrix products, apply_attn(): jnp.einsum('nhj,hij->nhi', v_heads, attn_weights, preferred_element_type=...  10.2 us
    dot_general x2, matrix products, project(): jnp.dot(normed, w_qkv, preferred_element_type=jnp.float32)  9.94 us
    dot_general x1, matrix products, local_step(): jnp.einsum('nk,ck->nc', d_qkv, w_qkv, preferred_element_type=jnp.float32)  6.45 us
    dot_general x1, matrix products, local_step(): jnp.einsum('nc,nk->ck', normed, d_qkv, preferred_element_type=jnp.float32)  6 us
  transfers between devices with their start and end apart: 4, of which 3 were waited for; matrix products, arithmetic and copies ran while one was open for 27% of the time, Pallas kernels for 0%

commit v1 on v0

v1 whole, which is shorter than its diff:
```python
import functools

import jax
import jax.numpy as jnp
from jax import lax
from jax.experimental import pallas as pl
from jax.experimental.pallas import tpu as pltpu
from jax.sharding import PartitionSpec as P

F32 = jnp.float32
BF16 = jnp.bfloat16
NN = (((1,), (0,)), ((), ()))
NT = (((1,), (1,)), ((), ()))
TN = (((0,), (0,)), ((), ()))
EPS = 1e-6


def mm(a, b, dims=NN):
    return lax.dot_general(a, b, dims, preferred_element_type=F32)


def kernel(ns, rows, width, heads, tile,
           x_hbm, dy_hbm, gain_hbm, bias_hbm, wqkv_hbm, wout_hbm, temp_ref,
           out_hbm, gtok_hbm, gwqkv_hbm, gwout_hbm, ggain_ref, gbias_ref, gtemp_ref,
           x_v, dy_v, gain_v, bias_v, wqkv_v, wout_v,
           u_v, q_v, k_v, v_v, do_v, o_v, dqkv_v, xhat_v, rstd_v,
           gacc, dacc, sqacc, skacc, gsend, grecv, dsend, drecv, a_all, e_all, st_all, bd_a, bd_g,
           gw, pre, opp, nrr, rlr, gwst, gbacc, gb_all,
           in_sem, out_sem, small_s, small_r, pre_s, pre_r, x2_s, x2_r):
    me = lax.axis_index('sp')
    nt = rows // tile
    hd = width // heads
    core = lax.rem(me, 2)
    chip = me // 2
    nchip = ns // 2
    partner = me + 1 - 2 * core
    right = lax.rem(me + 2, ns)
    left = lax.rem(me + ns - 2, ns)
    c_r = lax.rem(chip + 1, nchip)
    c_l = lax.rem(chip + nchip - 1, nchip)
    c_o = lax.rem(chip + 2, nchip)

    def remote(src, dst, ssem, rsem, dev):
        return pltpu.make_async_remote_copy(src_ref=src, dst_ref=dst, send_sem=ssem, recv_sem=rsem,
                                            device_id={'sp': dev}, device_id_type=pl.DeviceIdType.MESH)

    barrier = pltpu.get_barrier_semaphore()
    for r in range(1, ns):
        pl.semaphore_signal(barrier, inc=1, device_id={'sp': lax.rem(me + r, ns)},
                            device_id_type=pl.DeviceIdType.MESH)

    def ld(i, src, dst):
        return pltpu.make_async_copy(src, dst, in_sem.at[i])

    def tile_of(i):
        return pl.ds(pl.multiple_of(i * tile, tile), tile)

    def x_copy(i):
        return ld(i, x_hbm.at[tile_of(i)], x_v.at[tile_of(i)])

    def dy_copy(i):
        return ld(nt + i, dy_hbm.at[tile_of(i)], dy_v.at[tile_of(i)])

    gain_copy = ld(2 * nt, gain_hbm, gain_v)
    bias_copy = ld(2 * nt + 1, bias_hbm, bias_v)
    wqk_copy = ld(2 * nt + 2, wqkv_hbm.at[:, 0:2 * width], wqkv_v.at[:, 0:2 * width])
    wv_copy = ld(2 * nt + 3, wqkv_hbm.at[:, 2 * width:3 * width], wqkv_v.at[:, 2 * width:3 * width])
    wout_copy = ld(2 * nt + 4, wout_hbm, wout_v)
    gain_copy.start()
    bias_copy.start()
    x_copy(0).start()
    wqk_copy.start()
    for i in range(1, nt):
        x_copy(i).start()
    wv_copy.start()
    wout_copy.start()
    for i in range(nt):
        dy_copy(i).start()

    gacc[...] = jnp.zeros_like(gacc)
    dacc[...] = jnp.zeros_like(dacc)
    sqacc[...] = jnp.zeros_like(sqacc)
    skacc[...] = jnp.zeros_like(skacc)
    gbacc[...] = jnp.zeros_like(gbacc)
    bd_a[...] = jnp.zeros_like(bd_a)
    bd_g[...] = jnp.zeros_like(bd_g)
    gain_copy.wait()
    bias_copy.wait()
    wqk_copy.wait()

    ngrp = width // 256
    hpg = heads // ngrp

    def c1(i, carry):
        x_copy(i).wait()
        t = tile_of(i)
        x = x_v[t, :].astype(F32)
        mean = jnp.mean(x, axis=1, keepdims=True)
        cent = x - mean
        var = jnp.mean(cent * cent, axis=1, keepdims=True)
        rstd = lax.rsqrt(var + EPS)
        xhat = cent * rstd
        xhat_v[t, :] = xhat
        rstd_v[t, :] = rstd
        u = (xhat * gain_v[...] + bias_v[...]).astype(BF16)
        u_v[t, :] = u
        q = mm(u, wqkv_v[:, 0:width]).astype(BF16)
        q_v[t, :] = q
        k = mm(u, wqkv_v[:, width:2 * width]).astype(BF16)
        k_v[t, :] = k
        for g in range(ngrp):
            c = slice(256 * g, 256 * g + 256)
            gacc[g] += mm(q[:, c], k[:, c], TN)
        q32 = q.astype(F32)
        k32 = k.astype(F32)
        sqacc[...] += jnp.sum((q32 * q32).reshape(tile // 8, 8, width), axis=0)
        skacc[...] += jnp.sum((k32 * k32).reshape(tile // 8, 8, width), axis=0)
        return carry

    lax.fori_loop(0, nt, c1, 0)

    lane32 = lax.broadcasted_iota(jnp.int32, (hd // 2, 2 * hd), 1)

    def pack(acc, h):
        g, hh = h // hpg, h % hpg
        blk = acc[g, hh * hd:hh * hd + hd, (hh // 2) * 128:(hh // 2) * 128 + 128]
        top, bot = blk[0:hd // 2], blk[hd // 2:hd]
        if h % 2 == 0:
            bot = pltpu.roll(bot, hd, axis=1)
        else:
            top = pltpu.roll(top, hd, axis=1)
        return jnp.where(lane32 < hd, top, bot)

    sq_row = jnp.sum(sqacc[...], axis=0, keepdims=True)
    sk_row = jnp.sum(skacc[...], axis=0, keepdims=True)
    for h in range(heads):
        gsend[h, 0:hd // 2, :] = pack(gacc, h)
        c = slice((h // 2) * 128, (h // 2) * 128 + 128)
        gsend[h, hd // 2:hd // 2 + 1, :] = sq_row[:, c]
        gsend[h, hd // 2 + 1:hd // 2 + 2, :] = sk_row[:, c]

    def to_owner(kind, src, dst, r):
        dst_dev = lax.rem(me + r, ns)
        return remote(src.at[dst_dev], dst.at[r], small_s.at[kind, r], small_r.at[kind, r], dst_dev)

    def to_all(kind, buf, r):
        return remote(buf.at[me], buf.at[me], small_s.at[kind, r], small_r.at[kind, r], lax.rem(me + r, ns))

    pl.semaphore_wait(barrier, ns - 1)
    for r in range(1, ns):
        to_owner(0, gsend, grecv, r).start()

    wv_copy.wait()
    wout_copy.wait()

    def c2(i, carry):
        dy_copy(i).wait()
        t = tile_of(i)
        v = mm(u_v[t, :], wqkv_v[:, 2 * width:3 * width]).astype(BF16)
        v_v[t, :] = v
        do = mm(dy_v[t, :], wout_v[...], NT).astype(BF16)
        do_v[t, :] = do
        for g in range(ngrp):
            c = slice(256 * g, 256 * g + 256)
            dacc[g] += mm(do[:, c], v[:, c], TN)
        return carry

    lax.fori_loop(0, nt, c2, 0)
    for h in range(heads):
        dsend[h] = pack(dacc, h)
    for r in range(1, ns):
        to_owner(1, dsend, drecv, r).start()

    row = lax.broadcasted_iota(jnp.int32, (hd, 2 * hd), 0)
    lanep = lax.broadcasted_iota(jnp.int32, (hd, 2 * hd), 1) - hd * core
    half = (lanep >= 0) & (lanep < hd)
    diag = lanep == row
    half1 = half[0:1]

    def unpack(p):
        rolled = pltpu.roll(p, hd, axis=1)
        even = core == 0
        full = jnp.concatenate([jnp.where(even, p, rolled), jnp.where(even, rolled, p)], axis=0)
        return jnp.where(half, full, 0.0)

    for r in range(1, ns):
        to_owner(0, gsend, grecv, r).wait_recv()
    tot = gsend[me, 0:hd // 2 + 2]
    for r in range(1, ns):
        tot = tot + grecv[r, 0:hd // 2 + 2]
    gram = unpack(tot[0:hd // 2])
    sq_r = tot[hd // 2:hd // 2 + 1]
    sk_r = jnp.where(half1, tot[hd // 2 + 1:hd // 2 + 2], 1.0)
    sq_c = jnp.sum(jnp.where(diag, sq_r, 0.0), axis=1, keepdims=True)
    den = jnp.sqrt(sq_c) * jnp.sqrt(sk_r)
    cosine = gram / den
    temp = temp_ref[me]
    logits = jnp.where(half, temp * cosine, -jnp.inf)
    ex = jnp.exp(logits - jnp.max(logits, axis=1, keepdims=True))
    attn = ex / jnp.sum(ex, axis=1, keepdims=True)
    a_all[me] = attn.astype(BF16)
    for r in range(1, ns):
        to_all(2, a_all, r).start()

    for r in range(1, ns):
        to_owner(1, dsend, drecv, r).wait_recv()
    dtot = dsend[me]
    for r in range(1, ns):
        dtot = dtot + drecv[r]
    d_a = unpack(dtot)
    inner = jnp.sum(d_a * attn, axis=1, keepdims=True)
    d_s = attn * (d_a - inner)
    d_cos = temp * d_s
    d_t = jnp.sum(jnp.sum(d_s * cosine, axis=1, keepdims=True), axis=0, keepdims=True)
    e_all[me] = (d_cos / den).astype(BF16)
    ec = d_cos * cosine
    dsq_c = -0.5 * jnp.sum(ec, axis=1, keepdims=True) / sq_c
    dsk_r = -0.5 * jnp.sum(ec, axis=0, keepdims=True) / sk_r
    dsq_r = jnp.sum(jnp.where(diag, dsq_c, 0.0), axis=0, keepdims=True)
    st_all[me, 0:1, :] = dsq_r
    st_all[me, 1:2, :] = dsk_r
    st_all[me, 2:3, :] = jnp.broadcast_to(d_t, (1, 2 * hd))
    for r in range(1, ns):
        to_all(3, e_all, r).start()
    for r in range(1, ns):
        to_all(4, st_all, r).start()

    def fill(bd, blocks):
        for g in range(ngrp):
            for j in range(2):
                s = slice(128 * j, 128 * j + 128)
                h = g * hpg + 2 * j
                bd[g, s, s] = blocks[h:h + 2].reshape(128, 128)

    def pre_copy(pc):
        return remote(gw.at[pc, :, 1 - core], pre.at[pc], pre_s.at[pc], pre_r.at[pc], partner)

    hr = gw.shape[3] // 2
    lo, hi = slice(0, hr), slice(hr, 2 * hr)

    def first_copies(pc):
        return [remote(pre.at[pc, c_o, lo], opp.at[pc, 0], x2_s.at[pc, 0], x2_r.at[pc, 0], right),
                remote(pre.at[pc, c_o, hi], opp.at[pc, 1], x2_s.at[pc, 1], x2_r.at[pc, 1], left),
                remote(pre.at[pc, c_r, hi], nrr.at[pc, 0], x2_s.at[pc, 2], x2_r.at[pc, 2], right),
                remote(pre.at[pc, c_l, lo], nrr.at[pc, 1], x2_s.at[pc, 3], x2_r.at[pc, 3], left)]

    def relay_copies(pc):
        return [remote(pre.at[pc, c_r, lo], rlr.at[pc, 0], x2_s.at[pc, 4], x2_r.at[pc, 4], right),
                remote(pre.at[pc, c_l, hi], rlr.at[pc, 1], x2_s.at[pc, 5], x2_r.at[pc, 5], left)]

    def rs_pre(pc):
        pre_copy(pc).start()

    def rs_first(pc):
        pre_copy(pc).wait_recv()
        pre[pc] = pre[pc] + gw[pc, :, core]
        for cp in first_copies(pc):
            cp.start()

    def rs_relay(pc):
        first, second = first_copies(pc), relay_copies(pc)
        first[0].wait_recv()
        pre[pc, c_r, lo] = pre[pc, c_r, lo] + opp[pc, 0]
        second[0].start()
        first[1].wait_recv()
        pre[pc, c_l, hi] = pre[pc, c_l, hi] + opp[pc, 1]
        second[1].start()

    def rs_final(pc):
        first, second = first_copies(pc), relay_copies(pc)
        first[2].wait_recv()
        first[3].wait_recv()
        second[0].wait_recv()
        second[1].wait_recv()
        gwst[pc, lo] = pre[pc, chip, lo] + rlr[pc, 0] + nrr[pc, 1]
        gwst[pc, hi] = pre[pc, chip, hi] + nrr[pc, 0] + rlr[pc, 1]

    for r in range(1, ns):
        to_all(2, a_all, r).wait_recv()
    fill(bd_a, a_all)

    def c3(i, carry):
        t = tile_of(i)
        for g in range(ngrp):
            c = slice(256 * g, 256 * g + 256)
            o_v[t, c] = mm(v_v[t, c], bd_a[g], NT).astype(BF16)
        return carry

    lax.fori_loop(0, nt, c3, 0)
    gw[0] = mm(o_v[...], dy_v[...], TN).reshape(gw.shape[1:])
    rs_pre(0)

    def c4(i, carry):
        t = tile_of(i)
        for g in range(ngrp):
            c = slice(256 * g, 256 * g + 256)
            dqkv_v[t, 2 * width + 256 * g:2 * width + 256 * g + 256] = mm(do_v[t, c], bd_a[g]).astype(BF16)
        return carry

    lax.fori_loop(0, nt, c4, 0)
    gw[1] = mm(u_v[...], dqkv_v[:, 2 * width:3 * width], TN).reshape(gw.shape[1:])
    rs_pre(1)
    rs_first(0)

    for r in range(1, ns):
        to_all(3, e_all, r).wait_recv()
    for r in range(1, ns):
        to_all(4, st_all, r).wait_recv()
    fill(bd_g, e_all)
    pair = [st_all[2 * j, 0:2, :] + st_all[2 * j + 1, 0:2, :] for j in range(heads // 2)]
    dsq2 = jnp.concatenate([2.0 * p[0:1] for p in pair], axis=1)
    dsk2 = jnp.concatenate([2.0 * p[1:2] for p in pair], axis=1)
    lane1 = lax.broadcasted_iota(jnp.int32, (1, 2 * hd), 1)
    gt = jnp.zeros((1, 2 * hd), F32)
    for h in range(heads):
        gt = jnp.where(lane1 == h, st_all[h, 2:3, :], gt)
    gtemp_ref[...] = gt[:, 0:heads]

    def c5(i, carry):
        t = tile_of(i)
        for g in range(ngrp):
            c = slice(256 * g, 256 * g + 256)
            dqkv_v[t, c] = (mm(k_v[t, c], bd_g[g], NT) + q_v[t, c].astype(F32) * dsq2[:, c]).astype(BF16)
        return carry

    lax.fori_loop(0, nt, c5, 0)
    gw[2] = mm(u_v[...], dqkv_v[:, 0:width], TN).reshape(gw.shape[1:])
    rs_pre(2)
    rs_first(1)
    rs_relay(0)

    def c6(i, carry):
        t = tile_of(i)
        for g in range(ngrp):
            c = slice(256 * g, 256 * g + 256)
            dqkv_v[t, width + 256 * g:width + 256 * g + 256] = (
                mm(q_v[t, c], bd_g[g]) + k_v[t, c].astype(F32) * dsk2[:, c]).astype(BF16)
        return carry

    lax.fori_loop(0, nt, c6, 0)
    gw[3] = mm(u_v[...], dqkv_v[:, width:2 * width], TN).reshape(gw.shape[1:])
    rs_pre(3)
    rs_first(2)
    rs_relay(1)

    def out_copy(i):
        return pltpu.make_async_copy(x_v.at[tile_of(i)], out_hbm.at[tile_of(i)], out_sem.at[i])

    def gtok_copy(i):
        return pltpu.make_async_copy(dy_v.at[tile_of(i)], gtok_hbm.at[tile_of(i)], out_sem.at[nt + i])

    def c7(i, carry):
        t = tile_of(i)
        x_v[t, :] = (x_v[t, :].astype(F32) + mm(o_v[t, :], wout_v[...])).astype(BF16)
        out_copy(i).start()
        return carry

    def c8(i, carry):
        t = tile_of(i)
        du = mm(dqkv_v[t, :], wqkv_v[...], NT)
        xhat = xhat_v[t, :]
        p = du * xhat
        gbacc[0] += jnp.sum(p.reshape(tile // 8, 8, width), axis=0)
        gbacc[1] += jnp.sum(du.reshape(tile // 8, 8, width), axis=0)
        dxh = du * gain_v[...]
        m1 = jnp.mean(dxh, axis=1, keepdims=True)
        m2 = jnp.mean(p * gain_v[...], axis=1, keepdims=True)
        dx = rstd_v[t, :] * (dxh - m1 - xhat * m2)
        dy_v[t, :] = (dy_v[t, :].astype(F32) + dx).astype(BF16)
        gtok_copy(i).start()
        return carry

    lax.fori_loop(0, nt // 2, c8, 0)
    rs_first(3)
    rs_relay(2)
    lax.fori_loop(nt // 2, nt, c8, 0)

    gb_all[me, 0:1, :] = jnp.sum(gbacc[0], axis=0, keepdims=True)
    gb_all[me, 1:2, :] = jnp.sum(gbacc[1], axis=0, keepdims=True)
    for r in range(1, ns):
        to_all(5, gb_all, r).start()
    rs_relay(3)
    lax.fori_loop(0, nt, c7, 0)

    def gw_copy(pc):
        dst = gwout_hbm if pc == 0 else gwqkv_hbm.at[:, pl.ds({1: 2, 2: 0, 3: 1}[pc] * width, width)]
        return pltpu.make_async_copy(gwst.at[pc], dst, out_sem.at[2 * nt + pc])

    for pc in range(4):
        rs_final(pc)
        gw_copy(pc).start()

    for r in range(1, ns):
        to_all(5, gb_all, r).wait_recv()
    gb = gb_all[0, 0:2]
    for d in range(1, ns):
        gb = gb + gb_all[d, 0:2]
    ggain_ref[...] = gb[0:1]
    gbias_ref[...] = gb[1:2]

    for r in range(1, ns):
        to_owner(0, gsend, grecv, r).wait_send()
        to_owner(1, dsend, drecv, r).wait_send()
        to_all(2, a_all, r).wait_send()
        to_all(3, e_all, r).wait_send()
        to_all(4, st_all, r).wait_send()
        to_all(5, gb_all, r).wait_send()
    for pc in range(4):
        pre_copy(pc).wait_send()
        for cp in first_copies(pc) + relay_copies(pc):
            cp.wait_send()
        gw_copy(pc).wait()
    for i in range(nt):
        out_copy(i).wait()
        gtok_copy(i).wait()


def solution(mesh):
    ns = mesh.shape['sp']
    row_spec = P(('dp', 'sp'), None)
    part_spec = P('dp')

    def local_step(x, dy, gain, bias, w_qkv, w_out, temp):
        rows, width = x.shape
        heads = temp.shape[0]
        hd = width // heads
        tile = 512
        nt = rows // tile
        share = width // ns
        nchip = ns // 2
        ngrp = width // 256
        hbm = pl.BlockSpec(memory_space=pl.ANY)
        vmem = pl.BlockSpec(memory_space=pltpu.VMEM)
        tok = lambda: pltpu.VMEM((rows, width), BF16)
        outs = pl.pallas_call(
            functools.partial(kernel, ns, rows, width, heads, tile),
            out_shape=[jax.ShapeDtypeStruct((rows, width), BF16),
                       jax.ShapeDtypeStruct((rows, width), BF16),
                       jax.ShapeDtypeStruct((share, 3 * width), F32),
                       jax.ShapeDtypeStruct((share, width), F32),
                       jax.ShapeDtypeStruct((1, width), F32),
                       jax.ShapeDtypeStruct((1, width), F32),
                       jax.ShapeDtypeStruct((1, heads), F32)],
            in_specs=[hbm] * 6 + [pl.BlockSpec(memory_space=pltpu.SMEM)],
            out_specs=[hbm] * 4 + [vmem] * 3,
            scratch_shapes=[
                tok(), tok(), pltpu.VMEM((1, width), F32), pltpu.VMEM((1, width), F32),
                pltpu.VMEM((width, 3 * width), BF16), pltpu.VMEM((width, width), BF16),
                tok(), tok(), tok(), tok(), tok(), tok(), pltpu.VMEM((rows, 3 * width), BF16),
                pltpu.VMEM((rows, width), F32), pltpu.VMEM((rows, 1), F32),
                pltpu.VMEM((ngrp, 256, 256), F32), pltpu.VMEM((ngrp, 256, 256), F32),
                pltpu.VMEM((8, width), F32), pltpu.VMEM((8, width), F32),
                pltpu.VMEM((heads, hd // 2 + 8, 2 * hd), F32), pltpu.VMEM((ns, hd // 2 + 8, 2 * hd), F32),
                pltpu.VMEM((heads, hd // 2, 2 * hd), F32), pltpu.VMEM((ns, hd // 2, 2 * hd), F32),
                pltpu.VMEM((heads, hd, 2 * hd), BF16), pltpu.VMEM((heads, hd, 2 * hd), BF16),
                pltpu.VMEM((heads, 8, 2 * hd), F32),
                pltpu.VMEM((ngrp, 256, 256), BF16), pltpu.VMEM((ngrp, 256, 256), BF16),
                pltpu.VMEM((4, nchip, 2, share, width), F32), pltpu.VMEM((4, nchip, share, width), F32),
                pltpu.VMEM((4, 2, share // 2, width), F32), pltpu.VMEM((4, 2, share // 2, width), F32),
                pltpu.VMEM((4, 2, share // 2, width), F32), pltpu.VMEM((4, share, width), F32),
                pltpu.VMEM((2, 8, width), F32), pltpu.VMEM((ns, 8, width), F32),
                pltpu.SemaphoreType.DMA((2 * nt + 5,)), pltpu.SemaphoreType.DMA((2 * nt + 4,)),
                pltpu.SemaphoreType.DMA((6, ns)), pltpu.SemaphoreType.DMA((6, ns)),
                pltpu.SemaphoreType.DMA((4,)), pltpu.SemaphoreType.DMA((4,)),
                pltpu.SemaphoreType.DMA((4, 6)), pltpu.SemaphoreType.DMA((4, 6)),
            ],
            compiler_params=pltpu.CompilerParams(collective_id=0, has_side_effects=True,
                                                 vmem_limit_bytes=60 * 1024 * 1024),
        )(x, dy, gain.reshape(1, -1), bias.reshape(1, -1), w_qkv, w_out, temp)
        out, gtok, gwqkv, gwout, ggain, gbias, gtemp = outs
        return out, gtok, gwqkv, gwout, ggain.reshape(-1), gbias.reshape(-1), gtemp.reshape(-1)

    full = P()
    return jax.shard_map(local_step, mesh=mesh,
                         in_specs=(row_spec, row_spec, full, full, full, full, full),
                         out_specs=(row_spec, row_spec, row_spec, row_spec, part_spec, part_spec, part_spec),
                         check_vma=False)
```

time: 218 us -> 55.3 us (0.25)
  waiting for transfers between devices: 79 us -> 0 us
  matrix products: 63.5 us -> 0 us
  Pallas kernels: 0 us -> 46.9 us
  blocking collectives: 29.9 us -> 0 us
  other arithmetic: 25.5 us -> 0 us
  between operations: 14.1 us -> 0.68 us
  local copies, waits for them, and re-layouts: 5.38 us -> 7.61 us
    psum x2 -> x0, waiting for transfers between devices: 74.7 us -> none  [the longest x1 40.9 us: local_step(): d_probs = lax.psum(probs_part, 'sp')]
    dot_general x14 -> x0, matrix products: 63.5 us -> none  [the longest x2 10.2 us: apply_attn(): jnp.einsum('nhj,hij->nhi', v_heads, attn_weights, preferred_element_type=...]
    pallas_call x0 -> x1, Pallas kernels: none -> 46.9 us  [local_step(): pl.pallas_call(functools.partial(kernel, ns, rows, width, heads, tile), o...]
    psum x2 -> x0, blocking collectives: 29.9 us -> none  [the longest x1 16.1 us: local_step(): gram_sum, q_sq, k_sq = lax.psum((gram_part, qsq_part, ksq_part), 'sp')]
    reduce_sum x7 -> x0, other arithmetic: 13.3 us -> none  [the longest x2 4.96 us: layer_norm(): row_var = jnp.mean(centered * centered, axis=-1, keepdims=True)]
    convert_element_type x1 -> x0, other arithmetic: 5.26 us -> none  [local_step(): grad_tokens = (dy_loc.astype(jnp.float32) + d_x).astype(jnp.bfloat16)]
    sub x2 -> x0, other arithmetic: 4.15 us -> none  [attn_probs(): return jax.nn.softmax(value_a11[..., None, None] * cosine, axis=-1)]
    reduce_scatter x2 -> x0, waiting for transfers between devices: 4.07 us -> none  [the longest x1 4.07 us: local_step(): lax.psum_scatter(wqkv_part, 'sp', scatter_dimension=0, tiled=True)]
  transfers between devices with their start and end apart: 4 -> 0, of which waited for: 3 -> 0; matrix products, arithmetic and copies ran while one was open for 27% -> 0% of each run, Pallas kernels for 0% -> 0%
where the time goes in v1:
time: 55.3 us; the launch traced here: 55.2 us
  Pallas kernels  46.9 us (85%)
  local copies, waits for them, and re-layouts  7.61 us (14%)
  between operations  0.68 us (1%)
    pallas_call x1, Pallas kernels, local_step(): pl.pallas_call(functools.partial(kernel, ns, rows, width, heads, tile), o...  46.9 us
    unnamed x19, local copies, waits for them, and re-layouts  7.61 us

profile of v1, /device:TPU:112, one launch (start us, length us, event | category | flops | bytes accessed | tf_op | source)
XLA Modules:
  0.0 55.2 jit_solution(4708212808947973476)
XLA Ops:
  0.6 46.9 %shard_map.126 = (bf16[2048,512]{1,0:T(8,128)(2,1)}, bf16[2048,512]{1,0:T(8,128)(2,1)}, f32[64,1536]{1,0:T(8,128)}, f32[64,512]{1,0:T(8,128)}, f32[1,512]{1,0:T(...) custom-call(bf16[2048,512]{1,0:T(8,128)(2,1)} %x_hbm.1, bf16[2048,512]{1,0:T(8,128)(2,1)} %dy_hbm.1, f32[1,512]{1,0:T(1,128)} %bitcast.5, ...), custom_call_target="tpu_custom_call" | custom-call | tf_op jit(solution)/shard_map/pallas_call | solution.py:435
  47.5 0.0 copy-start
  47.6 3.2 %copy.21 = bf16[2048,512]{1,0:T(8,128)(2,1)} copy(bf16[2048,512]{1,0:T(8,128)(2,1)} %get-tuple-element.28) | data formatting | bytes 4194304
  50.7 0.0 copy-done
  50.7 0.0 copy-start.1
  50.8 0.0 copy-start.2
  50.8 0.0 copy-start.4
  50.8 0.0 copy-start.3
  50.8 0.0 copy-start.5
  50.8 1.3 %copy.22 = bf16[2048,512]{1,0:T(8,128)(2,1)} copy(bf16[2048,512]{1,0:T(8,128)(2,1)S(1)} %copy-done) | data formatting | bytes 4194304
  52.1 0.0 copy-done.1
  52.1 0.7 %copy.23 = f32[64,1536]{1,0:T(8,128)} copy(f32[64,1536]{1,0:T(8,128)S(1)} %copy-done.1) | data formatting | bytes 786432
  52.9 0.0 copy-done.2
  52.9 0.7 %copy.24 = f32[64,512]{1,0:T(8,128)} copy(f32[64,512]{1,0:T(8,128)S(1)} %copy-done.2) | data formatting | bytes 262144
  53.5 0.0 copy-done.4
  53.5 0.6 %copy.25 = f32[512]{0:T(512)} copy(f32[512]{0:T(512)S(1)} %bitcast.8) | data formatting | bytes 4096
  54.1 0.0 copy-done.3
  54.1 0.6 %copy.26 = f32[512]{0:T(512)} copy(f32[512]{0:T(512)S(1)} %bitcast.7) | data formatting | bytes 4096
  54.7 0.0 copy-done.5
  54.7 0.5 copy.27
Async XLA Ops:
  47.5 3.2 %copy-start = (bf16[2048,512]{1,0:T(8,128)(2,1)S(1)}, bf16[2048,512]{1,0:T(8,128)(2,1)}, u32[]{:S(2)}) copy-start(bf16[2048,512]{1,0:T(8,128)(2,1)} %get-tuple-element.29) | copy-start | bytes 6291460
  50.7 1.4 %copy-start.1 = (f32[64,1536]{1,0:T(8,128)S(1)}, f32[64,1536]{1,0:T(8,128)}, u32[]{:S(2)}) copy-start(f32[64,1536]{1,0:T(8,128)} %get-tuple-element.30) | copy-start | bytes 1179652
  50.8 2.1 %copy-start.2 = (f32[64,512]{1,0:T(8,128)S(1)}, f32[64,512]{1,0:T(8,128)}, u32[]{:S(2)}) copy-start(f32[64,512]{1,0:T(8,128)} %get-tuple-element.31) | copy-start | bytes 393220
  50.8 2.8 %copy-start.4 = (f32[1,512]{1,0:T(1,128)S(1)}, f32[1,512]{1,0:T(1,128)}, u32[]{:S(2)}) copy-start(f32[1,512]{1,0:T(1,128)} %get-tuple-element.18) | copy-start | bytes 6148
  50.8 3.3 %copy-start.3 = (f32[1,512]{1,0:T(1,128)S(1)}, f32[1,512]{1,0:T(1,128)}, u32[]{:S(2)}) copy-start(f32[1,512]{1,0:T(1,128)} %get-tuple-element.19) | copy-start | bytes 6148
  50.8 3.9 %copy-start.5 = (f32[1,8]{1,0:T(1,128)S(1)}, f32[1,8]{1,0:T(1,128)}, u32[]{:S(2)}) copy-start(f32[1,8]{1,0:T(1,128)} %get-tuple-element.20) | copy-start | bytes 100

commit v2 on v1

--- a/solution.py
+++ b/solution.py
@@ -21,12 +21,12 @@
 
 def kernel(ns, rows, width, heads, tile,
            x_hbm, dy_hbm, gain_hbm, bias_hbm, wqkv_hbm, wout_hbm, temp_ref,
-           out_hbm, gtok_hbm, gwqkv_hbm, gwout_hbm, ggain_ref, gbias_ref, gtemp_ref,
+           out_v, gtok_v, gwst, ggain_ref, gbias_ref, gtemp_ref,
            x_v, dy_v, gain_v, bias_v, wqkv_v, wout_v,
            u_v, q_v, k_v, v_v, do_v, o_v, dqkv_v, xhat_v, rstd_v,
            gacc, dacc, sqacc, skacc, gsend, grecv, dsend, drecv, a_all, e_all, st_all, bd_a, bd_g,
-           gw, pre, opp, nrr, rlr, gwst, gbacc, gb_all,
-           in_sem, out_sem, small_s, small_r, pre_s, pre_r, x2_s, x2_r):
+           gw, pre, opp, nrr, rlr, gbacc, gb_all,
+           in_sem, small_s, small_r, pre_s, pre_r, x2_s, x2_r):
     me = lax.axis_index('sp')
     nt = rows // tile
     hd = width // heads
@@ -77,16 +77,17 @@
     for i in range(nt):
         dy_copy(i).start()
 
-    gacc[...] = jnp.zeros_like(gacc)
-    dacc[...] = jnp.zeros_like(dacc)
-    sqacc[...] = jnp.zeros_like(sqacc)
-    skacc[...] = jnp.zeros_like(skacc)
-    gbacc[...] = jnp.zeros_like(gbacc)
-    bd_a[...] = jnp.zeros_like(bd_a)
-    bd_g[...] = jnp.zeros_like(bd_g)
-    gain_copy.wait()
-    bias_copy.wait()
-    wqk_copy.wait()
+    with jax.named_scope("init"):
+        gacc[...] = jnp.zeros_like(gacc)
+        dacc[...] = jnp.zeros_like(dacc)
+        sqacc[...] = jnp.zeros_like(sqacc)
+        skacc[...] = jnp.zeros_like(skacc)
+        gbacc[...] = jnp.zeros_like(gbacc)
+        bd_a[...] = jnp.zeros_like(bd_a)
+        bd_g[...] = jnp.zeros_like(bd_g)
+        gain_copy.wait()
+        bias_copy.wait()
+        wqk_copy.wait()
 
     ngrp = width // 256
     hpg = heads // ngrp
@@ -117,7 +118,8 @@
         skacc[...] += jnp.sum((k32 * k32).reshape(tile // 8, 8, width), axis=0)
         return carry
 
-    lax.fori_loop(0, nt, c1, 0)
+    with jax.named_scope("c1"):
+        lax.fori_loop(0, nt, c1, 0)
 
     lane32 = lax.broadcasted_iota(jnp.int32, (hd // 2, 2 * hd), 1)
 
@@ -131,13 +133,14 @@
             top = pltpu.roll(top, hd, axis=1)
         return jnp.where(lane32 < hd, top, bot)
 
-    sq_row = jnp.sum(sqacc[...], axis=0, keepdims=True)
-    sk_row = jnp.sum(skacc[...], axis=0, keepdims=True)
-    for h in range(heads):
-        gsend[h, 0:hd // 2, :] = pack(gacc, h)
-        c = slice((h // 2) * 128, (h // 2) * 128 + 128)
-        gsend[h, hd // 2:hd // 2 + 1, :] = sq_row[:, c]
-        gsend[h, hd // 2 + 1:hd // 2 + 2, :] = sk_row[:, c]
+    with jax.named_scope("packg"):
+        sq_row = jnp.sum(sqacc[...], axis=0, keepdims=True)
+        sk_row = jnp.sum(skacc[...], axis=0, keepdims=True)
+        for h in range(heads):
+            gsend[h, 0:hd // 2, :] = pack(gacc, h)
+            c = slice((h // 2) * 128, (h // 2) * 128 + 128)
+            gsend[h, hd // 2:hd // 2 + 1, :] = sq_row[:, c]
+            gsend[h, hd // 2 + 1:hd // 2 + 2, :] = sk_row[:, c]
 
     def to_owner(kind, src, dst, r):
         dst_dev = lax.rem(me + r, ns)
@@ -146,9 +149,10 @@
     def to_all(kind, buf, r):
         return remote(buf.at[me], buf.at[me], small_s.at[kind, r], small_r.at[kind, r], lax.rem(me + r, ns))
 
-    pl.semaphore_wait(barrier, ns - 1)
-    for r in range(1, ns):
-        to_owner(0, gsend, grecv, r).start()
+    with jax.named_scope("sendg"):
+        pl.semaphore_wait(barrier, ns - 1)
+        for r in range(1, ns):
+            to_owner(0, gsend, grecv, r).start()
 
     wv_copy.wait()
     wout_copy.wait()
@@ -165,11 +169,13 @@
             dacc[g] += mm(do[:, c], v[:, c], TN)
         return carry
 
-    lax.fori_loop(0, nt, c2, 0)
-    for h in range(heads):
-        dsend[h] = pack(dacc, h)
-    for r in range(1, ns):
-        to_owner(1, dsend, drecv, r).start()
+    with jax.named_scope("c2"):
+        lax.fori_loop(0, nt, c2, 0)
+    with jax.named_scope("sendd"):
+        for h in range(heads):
+            dsend[h] = pack(dacc, h)
+        for r in range(1, ns):
+            to_owner(1, dsend, drecv, r).start()
 
     row = lax.broadcasted_iota(jnp.int32, (hd, 2 * hd), 0)
     lanep = lax.broadcasted_iota(jnp.int32, (hd, 2 * hd), 1) - hd * core
@@ -183,47 +189,51 @@
         full = jnp.concatenate([jnp.where(even, p, rolled), jnp.where(even, rolled, p)], axis=0)
         return jnp.where(half, full, 0.0)
 
-    for r in range(1, ns):
-        to_owner(0, gsend, grecv, r).wait_recv()
-    tot = gsend[me, 0:hd // 2 + 2]
-    for r in range(1, ns):
-        tot = tot + grecv[r, 0:hd // 2 + 2]
-    gram = unpack(tot[0:hd // 2])
-    sq_r = tot[hd // 2:hd // 2 + 1]
-    sk_r = jnp.where(half1, tot[hd // 2 + 1:hd // 2 + 2], 1.0)
-    sq_c = jnp.sum(jnp.where(diag, sq_r, 0.0), axis=1, keepdims=True)
-    den = jnp.sqrt(sq_c) * jnp.sqrt(sk_r)
-    cosine = gram / den
-    temp = temp_ref[me]
-    logits = jnp.where(half, temp * cosine, -jnp.inf)
-    ex = jnp.exp(logits - jnp.max(logits, axis=1, keepdims=True))
-    attn = ex / jnp.sum(ex, axis=1, keepdims=True)
-    a_all[me] = attn.astype(BF16)
-    for r in range(1, ns):
-        to_all(2, a_all, r).start()
-
-    for r in range(1, ns):
-        to_owner(1, dsend, drecv, r).wait_recv()
-    dtot = dsend[me]
-    for r in range(1, ns):
-        dtot = dtot + drecv[r]
-    d_a = unpack(dtot)
-    inner = jnp.sum(d_a * attn, axis=1, keepdims=True)
-    d_s = attn * (d_a - inner)
-    d_cos = temp * d_s
-    d_t = jnp.sum(jnp.sum(d_s * cosine, axis=1, keepdims=True), axis=0, keepdims=True)
-    e_all[me] = (d_cos / den).astype(BF16)
-    ec = d_cos * cosine
-    dsq_c = -0.5 * jnp.sum(ec, axis=1, keepdims=True) / sq_c
-    dsk_r = -0.5 * jnp.sum(ec, axis=0, keepdims=True) / sk_r
-    dsq_r = jnp.sum(jnp.where(diag, dsq_c, 0.0), axis=0, keepdims=True)
-    st_all[me, 0:1, :] = dsq_r
-    st_all[me, 1:2, :] = dsk_r
-    st_all[me, 2:3, :] = jnp.broadcast_to(d_t, (1, 2 * hd))
-    for r in range(1, ns):
-        to_all(3, e_all, r).start()
-    for r in range(1, ns):
-        to_all(4, st_all, r).start()
+    with jax.named_scope("waitg"):
+        for r in range(1, ns):
+            to_owner(0, gsend, grecv, r).wait_recv()
+    with jax.named_scope("soft"):
+        tot = gsend[me, 0:hd // 2 + 2]
+        for r in range(1, ns):
+            tot = tot + grecv[r, 0:hd // 2 + 2]
+        gram = unpack(tot[0:hd // 2])
+        sq_r = tot[hd // 2:hd // 2 + 1]
+        sk_r = jnp.where(half1, tot[hd // 2 + 1:hd // 2 + 2], 1.0)
+        sq_c = jnp.sum(jnp.where(diag, sq_r, 0.0), axis=1, keepdims=True)
+        den = jnp.sqrt(sq_c) * jnp.sqrt(sk_r)
+        cosine = gram / den
+        temp = temp_ref[me]
+        logits = jnp.where(half, temp * cosine, -jnp.inf)
+        ex = jnp.exp(logits - jnp.max(logits, axis=1, keepdims=True))
+        attn = ex / jnp.sum(ex, axis=1, keepdims=True)
+        a_all[me] = attn.astype(BF16)
+        for r in range(1, ns):
+            to_all(2, a_all, r).start()
+
+    with jax.named_scope("waitd"):
+        for r in range(1, ns):
+            to_owner(1, dsend, drecv, r).wait_recv()
+    with jax.named_scope("vjp"):
+        dtot = dsend[me]
+        for r in range(1, ns):
+            dtot = dtot + drecv[r]
+        d_a = unpack(dtot)
+        inner = jnp.sum(d_a * attn, axis=1, keepdims=True)
+        d_s = attn * (d_a - inner)
+        d_cos = temp * d_s
+        d_t = jnp.sum(jnp.sum(d_s * cosine, axis=1, keepdims=True), axis=0, keepdims=True)
+        e_all[me] = (d_cos / den).astype(BF16)
+        ec = d_cos * cosine
+        dsq_c = -0.5 * jnp.sum(ec, axis=1, keepdims=True) / sq_c
+        dsk_r = -0.5 * jnp.sum(ec, axis=0, keepdims=True) / sk_r
+        dsq_r = jnp.sum(jnp.where(diag, dsq_c, 0.0), axis=0, keepdims=True)
+        st_all[me, 0:1, :] = dsq_r
+        st_all[me, 1:2, :] = dsk_r
+        st_all[me, 2:3, :] = jnp.broadcast_to(d_t, (1, 2 * hd))
+        for r in range(1, ns):
+            to_all(3, e_all, r).start()
+        for r in range(1, ns):
+            to_all(4, st_all, r).start()
 
     def fill(bd, blocks):
         for g in range(ngrp):
@@ -275,8 +285,9 @@
         gwst[pc, lo] = pre[pc, chip, lo] + rlr[pc, 0] + nrr[pc, 1]
         gwst[pc, hi] = pre[pc, chip, hi] + nrr[pc, 0] + rlr[pc, 1]
 
-    for r in range(1, ns):
-        to_all(2, a_all, r).wait_recv()
+    with jax.named_scope("waita"):
+        for r in range(1, ns):
+            to_all(2, a_all, r).wait_recv()
     fill(bd_a, a_all)
 
     def c3(i, carry):
@@ -286,9 +297,11 @@
             o_v[t, c] = mm(v_v[t, c], bd_a[g], NT).astype(BF16)
         return carry
 
-    lax.fori_loop(0, nt, c3, 0)
-    gw[0] = mm(o_v[...], dy_v[...], TN).reshape(gw.shape[1:])
-    rs_pre(0)
+    with jax.named_scope("c3"):
+        lax.fori_loop(0, nt, c3, 0)
+    with jax.named_scope("gw0"):
+        gw[0] = mm(o_v[...], dy_v[...], TN).reshape(gw.shape[1:])
+        rs_pre(0)
 
     def c4(i, carry):
         t = tile_of(i)
@@ -297,15 +310,19 @@
             dqkv_v[t, 2 * width + 256 * g:2 * width + 256 * g + 256] = mm(do_v[t, c], bd_a[g]).astype(BF16)
         return carry
 
-    lax.fori_loop(0, nt, c4, 0)
-    gw[1] = mm(u_v[...], dqkv_v[:, 2 * width:3 * width], TN).reshape(gw.shape[1:])
-    rs_pre(1)
-    rs_first(0)
-
-    for r in range(1, ns):
-        to_all(3, e_all, r).wait_recv()
-    for r in range(1, ns):
-        to_all(4, st_all, r).wait_recv()
+    with jax.named_scope("c4"):
+        lax.fori_loop(0, nt, c4, 0)
+    with jax.named_scope("gw1"):
+        gw[1] = mm(u_v[...], dqkv_v[:, 2 * width:3 * width], TN).reshape(gw.shape[1:])
+        rs_pre(1)
+    with jax.named_scope("first0"):
+        rs_first(0)
+
+    with jax.named_scope("waite"):
+        for r in range(1, ns):
+            to_all(3, e_all, r).wait_recv()
+        for r in range(1, ns):
+            to_all(4, st_all, r).wait_recv()
     fill(bd_g, e_all)
     pair = [st_all[2 * j, 0:2, :] + st_all[2 * j + 1, 0:2, :] for j in range(heads // 2)]
     dsq2 = jnp.concatenate([2.0 * p[0:1] for p in pair], axis=1)
@@ -323,11 +340,14 @@
             dqkv_v[t, c] = (mm(k_v[t, c], bd_g[g], NT) + q_v[t, c].astype(F32) * dsq2[:, c]).astype(BF16)
         return carry
 
-    lax.fori_loop(0, nt, c5, 0)
-    gw[2] = mm(u_v[...], dqkv_v[:, 0:width], TN).reshape(gw.shape[1:])
-    rs_pre(2)
-    rs_first(1)
-    rs_relay(0)
+    with jax.named_scope("c5"):
+        lax.fori_loop(0, nt, c5, 0)
+    with jax.named_scope("gw2"):
+        gw[2] = mm(u_v[...], dqkv_v[:, 0:width], TN).reshape(gw.shape[1:])
+        rs_pre(2)
+    with jax.named_scope("first1relay0"):
+        rs_first(1)
+        rs_relay(0)
 
     def c6(i, carry):
         t = tile_of(i)
@@ -337,22 +357,18 @@
                 mm(q_v[t, c], bd_g[g]) + k_v[t, c].astype(F32) * dsk2[:, c]).astype(BF16)
         return carry
 
-    lax.fori_loop(0, nt, c6, 0)
-    gw[3] = mm(u_v[...], dqkv_v[:, width:2 * width], TN).reshape(gw.shape[1:])
-    rs_pre(3)
-    rs_first(2)
-    rs_relay(1)
-
-    def out_copy(i):
-        return pltpu.make_async_copy(x_v.at[tile_of(i)], out_hbm.at[tile_of(i)], out_sem.at[i])
-
-    def gtok_copy(i):
-        return pltpu.make_async_copy(dy_v.at[tile_of(i)], gtok_hbm.at[tile_of(i)], out_sem.at[nt + i])
+    with jax.named_scope("c6"):
+        lax.fori_loop(0, nt, c6, 0)
+    with jax.named_scope("gw3"):
+        gw[3] = mm(u_v[...], dqkv_v[:, width:2 * width], TN).reshape(gw.shape[1:])
+        rs_pre(3)
+    with jax.named_scope("first2relay1"):
+        rs_first(2)
+        rs_relay(1)
 
     def c7(i, carry):
         t = tile_of(i)
-        x_v[t, :] = (x_v[t, :].astype(F32) + mm(o_v[t, :], wout_v[...])).astype(BF16)
-        out_copy(i).start()
+        out_v[t, :] = (x_v[t, :].astype(F32) + mm(o_v[t, :], wout_v[...])).astype(BF16)
         return carry
 
     def c8(i, carry):
@@ -366,53 +382,60 @@
         m1 = jnp.mean(dxh, axis=1, keepdims=True)
         m2 = jnp.mean(p * gain_v[...], axis=1, keepdims=True)
         dx = rstd_v[t, :] * (dxh - m1 - xhat * m2)
-        dy_v[t, :] = (dy_v[t, :].astype(F32) + dx).astype(BF16)
-        gtok_copy(i).start()
-        return carry
-
-    lax.fori_loop(0, nt // 2, c8, 0)
-    rs_first(3)
-    rs_relay(2)
-    lax.fori_loop(nt // 2, nt, c8, 0)
+        gtok_v[t, :] = (dy_v[t, :].astype(F32) + dx).astype(BF16)
+        return carry
+
+    with jax.named_scope("c8a"):
+        lax.fori_loop(0, nt // 2, c8, 0)
+    with jax.named_scope("first3relay2"):
+        rs_first(3)
+        rs_relay(2)
+    with jax.named_scope("c8b"):
+        lax.fori_loop(nt // 2, nt, c8, 0)
 
     gb_all[me, 0:1, :] = jnp.sum(gbacc[0], axis=0, keepdims=True)
     gb_all[me, 1:2, :] = jnp.sum(gbacc[1], axis=0, keepdims=True)
     for r in range(1, ns):
         to_all(5, gb_all, r).start()
-    rs_relay(3)
-    lax.fori_loop(0, nt, c7, 0)
-
-    def gw_copy(pc):
-        dst = gwout_hbm if pc == 0 else gwqkv_hbm.at[:, pl.ds({1: 2, 2: 0, 3: 1}[pc] * width, width)]
-        return pltpu.make_async_copy(gwst.at[pc], dst, out_sem.at[2 * nt + pc])
-
-    for pc in range(4):
-        rs_final(pc)
-        gw_copy(pc).start()
-
-    for r in range(1, ns):
-        to_all(5, gb_all, r).wait_recv()
-    gb = gb_all[0, 0:2]
-    for d in range(1, ns):
-        gb = gb + gb_all[d, 0:2]
-    ggain_ref[...] = gb[0:1]
-    gbias_ref[...] = gb[1:2]
-
-    for r in range(1, ns):
-        to_owner(0, gsend, grecv, r).wait_send()
-        to_owner(1, dsend, drecv, r).wait_send()
-        to_all(2, a_all, r).wait_send()
-        to_all(3, e_all, r).wait_send()
-        to_all(4, st_all, r).wait_send()
-        to_all(5, gb_all, r).wait_send()
-    for pc in range(4):
-        pre_copy(pc).wait_send()
-        for cp in first_copies(pc) + relay_copies(pc):
-            cp.wait_send()
-        gw_copy(pc).wait()
-    for i in range(nt):
-        out_copy(i).wait()
-        gtok_copy(i).wait()
+    with jax.named_scope("relay3"):
+        rs_relay(3)
+    with jax.named_scope("c7"):
+        lax.fori_loop(0, nt, c7, 0)
+
+    with jax.named_scope("final"):
+        for pc in range(4):
+            rs_final(pc)
+
+    with jax.named_scope("gb"):
+        for r in range(1, ns):
+            to_all(5, gb_all, r).wait_recv()
+        gb = gb_all[0, 0:2]
+        for d in range(1, ns):
+            gb = gb + gb_all[d, 0:2]
+        ggain_ref[...] = gb[0:1]
+        gbias_ref[...] = gb[1:2]
+
+    with jax.named_scope("drain"):
+        for r in range(1, ns):
+            to_owner(0, gsend, grecv, r).wait_send()
+            to_owner(1, dsend, drecv, r).wait_send()
+            to_all(2, a_all, r).wait_send()
+            to_all(3, e_all, r).wait_send()
+            to_all(4, st_all, r).wait_send()
+            to_all(5, gb_all, r).wait_send()
+        for pc in range(4):
+            pre_copy(pc).wait_send()
+            for cp in first_copies(pc) + relay_copies(pc):
+                cp.wait_send()
+
+
+def writer(width, out_v, gtok_v, gwst, gg_v, gb_v, gt_v, out_hbm, gtok_hbm, gwqkv_hbm, gwout_hbm, gg_hbm, gb_hbm, gt_hbm, sem):
+    copies = [(out_v, out_hbm), (gtok_v, gtok_hbm), (gwst.at[0], gwout_hbm), (gg_v, gg_hbm), (gb_v, gb_hbm), (gt_v, gt_hbm)]
+    copies += [(gwst.at[pc], gwqkv_hbm.at[:, pl.ds(c * width, width)]) for pc, c in ((1, 2), (2, 0), (3, 1))]
+    for i, (src, dst) in enumerate(copies):
+        pltpu.make_async_copy(src, dst, sem.at[i]).start()
+    for i, (src, dst) in enumerate(copies):
+        pltpu.make_async_copy(src, dst, sem.at[i]).wait()
 
 
 def solution(mesh):
@@ -434,15 +457,11 @@
         tok = lambda: pltpu.VMEM((rows, width), BF16)
         outs = pl.pallas_call(
             functools.partial(kernel, ns, rows, width, heads, tile),
-            out_shape=[jax.ShapeDtypeStruct((rows, width), BF16),
-                       jax.ShapeDtypeStruct((rows, width), BF16),
-                       jax.ShapeDtypeStruct((share, 3 * width), F32),
-                       jax.ShapeDtypeStruct((share, width), F32),
-                       jax.ShapeDtypeStruct((1, width), F32),
-                       jax.ShapeDtypeStruct((1, width), F32),
-                       jax.ShapeDtypeStruct((1, heads), F32)],
+            out_shape=[pltpu.VMEM((rows, width), BF16), pltpu.VMEM((rows, width), BF16),
+                       pltpu.VMEM((4, share, width), F32), pltpu.VMEM((1, width), F32),
+                       pltpu.VMEM((1, width), F32), pltpu.VMEM((1, heads), F32)],
             in_specs=[hbm] * 6 + [pl.BlockSpec(memory_space=pltpu.SMEM)],
-            out_specs=[hbm] * 4 + [vmem] * 3,
+            out_specs=[vmem] * 6,
             scratch_shapes=[
                 tok(), tok(), pltpu.VMEM((1, width), F32), pltpu.VMEM((1, width), F32),
                 pltpu.VMEM((width, 3 * width), BF16), pltpu.VMEM((width, width), BF16),
@@ -457,17 +476,30 @@
                 pltpu.VMEM((ngrp, 256, 256), BF16), pltpu.VMEM((ngrp, 256, 256), BF16),
                 pltpu.VMEM((4, nchip, 2, share, width), F32), pltpu.VMEM((4, nchip, share, width), F32),
                 pltpu.VMEM((4, 2, share // 2, width), F32), pltpu.VMEM((4, 2, share // 2, width), F32),
-                pltpu.VMEM((4, 2, share // 2, width), F32), pltpu.VMEM((4, share, width), F32),
+                pltpu.VMEM((4, 2, share // 2, width), F32),
                 pltpu.VMEM((2, 8, width), F32), pltpu.VMEM((ns, 8, width), F32),
-                pltpu.SemaphoreType.DMA((2 * nt + 5,)), pltpu.SemaphoreType.DMA((2 * nt + 4,)),
+                pltpu.SemaphoreType.DMA((2 * nt + 5,)),
                 pltpu.SemaphoreType.DMA((6, ns)), pltpu.SemaphoreType.DMA((6, ns)),
                 pltpu.SemaphoreType.DMA((4,)), pltpu.SemaphoreType.DMA((4,)),
                 pltpu.SemaphoreType.DMA((4, 6)), pltpu.SemaphoreType.DMA((4, 6)),
             ],
             compiler_params=pltpu.CompilerParams(collective_id=0, has_side_effects=True,
-                                                 vmem_limit_bytes=60 * 1024 * 1024),
+                                                 vmem_limit_bytes=52 * 1024 * 1024),
         )(x, dy, gain.reshape(1, -1), bias.reshape(1, -1), w_qkv, w_out, temp)
-        out, gtok, gwqkv, gwout, ggain, gbias, gtemp = outs
+        out, gtok, gwqkv, gwout, ggain, gbias, gtemp = pl.pallas_call(
+            functools.partial(writer, width),
+            out_shape=[jax.ShapeDtypeStruct((rows, width), BF16),
+                       jax.ShapeDtypeStruct((rows, width), BF16),
+                       jax.ShapeDtypeStruct((share, 3 * width), F32),
+                       jax.ShapeDtypeStruct((share, width), F32),
+                       jax.ShapeDtypeStruct((1, width), F32),
+                       jax.ShapeDtypeStruct((1, width), F32),
+                       jax.ShapeDtypeStruct((1, heads), F32)],
+            in_specs=[vmem] * 6,
+            out_specs=[hbm] * 7,
+            scratch_shapes=[pltpu.SemaphoreType.DMA((9,))],
+            compiler_params=pltpu.CompilerParams(vmem_limit_bytes=1024 * 1024),
+        )(*outs)
         return out, gtok, gwqkv, gwout, ggain.reshape(-1), gbias.reshape(-1), gtemp.reshape(-1)
 
     full = P()

time: 55.3 us -> 48.7 us (0.88)
  local copies, waits for them, and re-layouts: 7.61 us -> 0 us
  Pallas kernels: 46.9 us -> 48 us
    unnamed x19 -> x0, local copies, waits for them, and re-layouts: 7.61 us -> none
    pallas_call x0 -> x1, Pallas kernels: none -> 2.25 us  [local_step(): pl.pallas_call(functools.partial(writer, width), out_shape=[jax.ShapeDtyp...]
    pallas_call x1, Pallas kernels: 46.9 us -> 45.7 us  [local_step(): pl.pallas_call(functools.partial(kernel, ns, rows, width, heads, tile), o...]
where the time goes in v2:
time: 48.7 us; the launch traced here: 48.6 us
  Pallas kernels  48 us (99%)
  between operations  0.64 us (1%)
    pallas_call x1, Pallas kernels, local_step(): pl.pallas_call(functools.partial(kernel, ns, rows, width, heads, tile), o...  45.7 us
    pallas_call x1, Pallas kernels, local_step(): pl.pallas_call(functools.partial(writer, width), out_shape=[jax.ShapeDtyp...  2.25 us

profile of v2, /device:TPU:112, one launch (start us, length us, event | category | flops | bytes accessed | tf_op | source)
XLA Modules:
  0.0 48.6 jit_solution(11584892360085190479)
XLA Ops:
  0.6 45.7 %shard_map.126 = (bf16[2048,512]{1,0:T(8,128)(2,1)S(1)}, bf16[2048,512]{1,0:T(8,128)(2,1)S(1)}, f32[4,64,512]{2,1,0:T(8,128)S(1)}, f32[1,512]{1,0:T(1,128)S(1)},...) custom-call(bf16[2048,512]{1,0:T(8,128)(2,1)} %x_hbm.1, bf16[2048,512]{1,0:T(8,128)(2,1)} %dy_hbm.1, f32[1,512]{1,0:T(1,128)} %bitcast.5, ...), custom_call_target="tpu_custom_call" | custom-call | tf_op jit(solution)/shard_map/pallas_call | solution.py:458
  46.4 2.2 %shard_map.127 = (bf16[2048,512]{1,0:T(8,128)(2,1)}, bf16[2048,512]{1,0:T(8,128)(2,1)}, f32[64,1536]{1,0:T(8,128)}, f32[64,512]{1,0:T(8,128)}, f32[1,512]{1,0:T(...) custom-call(bf16[2048,512]{1,0:T(8,128)(2,1)S(1)} %get-tuple-element.20.out_v, bf16[2048,512]{1,0:T(8,128)(2,1)S(1)} %get-tuple-element.21.gtok_v, ...), custom_call_target="tpu_custom_call" | custom-call | tf_op jit(solution)/shard_map/pallas_call | solution.py:489

commit v3 on v0

v3 whole, which is shorter than its diff:
```python
import functools

import jax
import jax.numpy as jnp
from jax import lax
from jax.experimental import pallas as pl
from jax.experimental.pallas import tpu as pltpu
from jax.sharding import PartitionSpec as P

F32 = jnp.float32
BF16 = jnp.bfloat16
NN = (((1,), (0,)), ((), ()))
NT = (((1,), (1,)), ((), ()))
TN = (((0,), (0,)), ((), ()))
EPS = 1e-6


def mm(a, b, dims=NN):
    return lax.dot_general(a, b, dims, preferred_element_type=F32)


def kernel(ns, rows, width, heads, tile,
           x_hbm, dy_hbm, gain_hbm, bias_hbm, wqkv_hbm, wout_hbm, temp_ref,
           out_v, gtok_v, gwst, ggain_ref, gbias_ref, gtemp_ref,
           x_v, dy_v, gain_v, bias_v, wqkv_v, wout_v,
           u_v, q_v, k_v, v_v, do_v, o_v, dqkv_v, mean_v, rstd_v,
           gacc, dacc, sqacc, skacc, gsend, gpre, grecv, dsend, dpre, drecv, a_all, e_all, st_all, bd_a, bd_g,
           gw, pre, opp, fin, gbacc, gb_all,
           in_sem, own_s, own_r, all_s, all_r, pre_s, pre_r, opp_s, opp_r, fin_s, fin_r):
    me = lax.axis_index('sp')
    nt = rows // tile
    hd = width // heads
    core = lax.rem(me, 2)
    chip = me // 2
    nchip = ns // 2
    partner = me + 1 - 2 * core
    right = lax.rem(me + 2, ns)
    left = lax.rem(me + ns - 2, ns)
    c_r = lax.rem(chip + 1, nchip)
    c_l = lax.rem(chip + nchip - 1, nchip)
    c_o = lax.rem(chip + 2, nchip)
    scope = jax.named_scope

    def remote(src, dst, ssem, rsem, dev):
        return lambda: pltpu.make_async_remote_copy(src_ref=src, dst_ref=dst, send_sem=ssem, recv_sem=rsem,
                                                    device_id={'sp': dev}, device_id_type=pl.DeviceIdType.MESH)

    def wait_bytes(ref, sem):
        pltpu.make_async_copy(ref, ref, sem).wait()

    far_first = sorted(range(1, nchip), key=lambda s: -min(s, nchip - s))
    peers = [2 * lax.rem(chip + s, nchip) + c for s in far_first for c in (core, 1 - core)] + [partner]

    barrier = pltpu.get_barrier_semaphore()
    for dev in peers:
        pl.semaphore_signal(barrier, inc=1, device_id={'sp': dev}, device_id_type=pl.DeviceIdType.MESH)

    def ld(i, src, dst):
        return lambda: pltpu.make_async_copy(src, dst, in_sem.at[i])

    def tile_of(i):
        return slice(i * tile, (i + 1) * tile)

    def x_copy(i):
        return ld(i, x_hbm.at[tile_of(i)], x_v.at[tile_of(i)])

    dy_copy = ld(nt, dy_hbm, dy_v)
    gain_copy = ld(nt + 1, gain_hbm, gain_v)
    bias_copy = ld(nt + 2, bias_hbm, bias_v)
    wqk_copy = ld(nt + 3, wqkv_hbm.at[:, 0:2 * width], wqkv_v.at[:, 0:2 * width])
    wv_copy = ld(nt + 4, wqkv_hbm.at[:, 2 * width:3 * width], wqkv_v.at[:, 2 * width:3 * width])
    wout_copy = ld(nt + 5, wout_hbm, wout_v)
    gain_copy().start()
    bias_copy().start()
    x_copy(0)().start()
    wqk_copy().start()
    for i in range(1, nt):
        x_copy(i)().start()
    wv_copy().start()
    wout_copy().start()
    dy_copy().start()

    with scope('init'):
        bd_a[...] = jnp.zeros_like(bd_a)
        bd_g[...] = jnp.zeros_like(bd_g)
        gain_copy().wait()
        bias_copy().wait()

    ngrp = width // 256
    hpg = heads // ngrp

    def cols(g):
        return slice(256 * g, 256 * g + 256)

    def ln(t):
        x = x_v[t, :].astype(F32)
        mean = jnp.mean(x, axis=1, keepdims=True)
        cent = x - mean
        var = jnp.mean(cent * cent, axis=1, keepdims=True)
        rstd = lax.rsqrt(var + EPS)
        mean_v[t, :] = mean
        rstd_v[t, :] = rstd
        u_v[t, :] = (cent * rstd * gain_v[...] + bias_v[...]).astype(BF16)

    def accumulate(ref, idx, val, first):
        if first:
            ref[idx] = val
        else:
            ref[idx] += val

    def square_sum(ref, c, val, first):
        v32 = val.astype(F32)
        part = jnp.sum((v32 * v32).reshape(tile // 8, 8, 256), axis=0)
        ref[:, c] = part if first else ref[:, c] + part

    nsub = 2 * ngrp
    sub = tile // nsub

    def ln_sub(i, j):
        if i < nt:
            ln(slice(i * tile + j * sub, i * tile + (j + 1) * sub))

    with scope('c1'):
        x_copy(0)().wait()
        for j in range(nsub):
            ln_sub(0, j)
        wqk_copy().wait()
        for i in range(1, nt):
            x_copy(i)().wait()
        for i in range(nt):
            t = tile_of(i)
            for g in range(ngrp):
                c = cols(g)
                q = mm(u_v[t, :], wqkv_v[:, c]).astype(BF16)
                q_v[t, c] = q
                square_sum(sqacc, c, q, i == 0)
                ln_sub(i + 1, 2 * g)
                k = mm(u_v[t, :], wqkv_v[:, width + 256 * g:width + 256 * g + 256]).astype(BF16)
                k_v[t, c] = k
                square_sum(skacc, c, k, i == 0)
                ln_sub(i + 1, 2 * g + 1)
                accumulate(gacc, g, mm(q, k, TN), i == 0)

    lane32 = lax.broadcasted_iota(jnp.int32, (hd // 2, 2 * hd), 1)

    def pack_block(blk, odd):
        top, bot = blk[0:hd // 2], blk[hd // 2:hd]
        if odd:
            top = pltpu.roll(top, hd, axis=1)
        else:
            bot = pltpu.roll(bot, hd, axis=1)
        return jnp.where(lane32 < hd, top, bot)

    def pack(acc, h):
        g, hh = h // hpg, h % hpg
        return pack_block(acc[g, hh * hd:hh * hd + hd, (hh // 2) * 128:(hh // 2) * 128 + 128], h % 2 == 1)

    with scope('packg'):
        sq_row = jnp.sum(sqacc[...], axis=0, keepdims=True)
        sk_row = jnp.sum(skacc[...], axis=0, keepdims=True)
        for h in range(heads):
            gsend[h // 2, h % 2, 0:hd // 2, :] = pack(gacc, h)
            c = slice((h // 2) * 128, (h // 2) * 128 + 128)
            gsend[h // 2, h % 2, hd // 2:hd // 2 + 1, :] = sq_row[:, c]
            gsend[h // 2, h % 2, hd // 2 + 1:hd // 2 + 2, :] = sk_row[:, c]

    def to_partner(kind, src, dst):
        return remote(src.at[:, 1 - core], dst, own_s.at[kind, 0], own_r.at[kind, 0], partner)

    def chip_sum(kind, src, mid, dst):
        wait_bytes(mid, own_r.at[kind, 0])
        n = mid.shape[1] if kind else hd // 2 + 2
        for c in range(nchip):
            mid[c, 0:n] = mid[c, 0:n] + src[c, core, 0:n]
        for s in far_first:
            c = lax.rem(chip + s, nchip)
            remote(mid.at[c], dst.at[s], own_s.at[kind, 1], own_r.at[kind, 1], 2 * c + core)().start()

    def image_sum(kind, mid, dst):
        n = mid.shape[1] if kind else hd // 2 + 2
        wait_bytes(dst.at[1:nchip], own_r.at[kind, 1])
        tot = mid[chip, 0:n]
        for s in range(1, nchip):
            tot = tot + dst[s, 0:n]
        return tot

    def to_all(kind, buf):
        for dev in peers:
            remote(buf.at[me], buf.at[me], all_s.at[kind], all_r.at[kind], dev)().start()

    def from_all(kind, buf):
        wait_bytes(buf.at[0:ns - 1], all_r.at[kind])

    with scope('sendg'):
        pl.semaphore_wait(barrier, ns - 1)
        to_partner(0, gsend, gpre)().start()

    def c2(i):
        t = tile_of(i)
        v = mm(u_v[t, :], wqkv_v[:, 2 * width:3 * width]).astype(BF16)
        v_v[t, :] = v
        do = mm(dy_v[t, :], wout_v[...], NT).astype(BF16)
        do_v[t, :] = do
        for g in range(ngrp):
            accumulate(dacc, g, mm(do[:, cols(g)], v[:, cols(g)], TN), i == 0)

    with scope('c2a'):
        wv_copy().wait()
        wout_copy().wait()
        dy_copy().wait()
        c2(0)
    with scope('chipg'):
        chip_sum(0, gsend, gpre, grecv)
    with scope('c2b'):
        for i in range(1, nt):
            c2(i)
    with scope('sendd'):
        for h in range(heads):
            dsend[h // 2, h % 2] = pack(dacc, h)
        to_partner(1, dsend, dpre)().start()

    row = lax.broadcasted_iota(jnp.int32, (hd, 2 * hd), 0)
    lanep = lax.broadcasted_iota(jnp.int32, (hd, 2 * hd), 1) - hd * core
    half = (lanep >= 0) & (lanep < hd)
    diag = lanep == row
    half1 = half[0:1]
    even = core == 0

    def unpack(p):
        rolled = pltpu.roll(p, hd, axis=1)
        full = jnp.concatenate([jnp.where(even, p, rolled), jnp.where(even, rolled, p)], axis=0)
        return jnp.where(half, full, 0.0)

    def pack_mine(blk):
        rolled = pltpu.roll(blk, hd, axis=1)
        low, high = jnp.where(even, blk, rolled), jnp.where(even, rolled, blk)
        return jnp.where(lane32 < hd, low[0:hd // 2], high[hd // 2:hd])

    with scope('waitg'):
        tot = image_sum(0, gpre, grecv)
    with scope('soft'):
        gram = unpack(tot[0:hd // 2])
        sq_r = tot[hd // 2:hd // 2 + 1]
        sk_r = jnp.where(half1, tot[hd // 2 + 1:hd // 2 + 2], 1.0)
        sq_c = jnp.sum(jnp.where(diag, sq_r, 0.0), axis=1, keepdims=True)
        den = jnp.sqrt(sq_c) * jnp.sqrt(sk_r)
        cosine = gram / den
        temp = temp_ref[me]
        logits = jnp.where(half, temp * cosine, -jnp.inf)
        ex = jnp.exp(logits - jnp.max(logits, axis=1, keepdims=True))
        attn = ex / jnp.sum(ex, axis=1, keepdims=True)
        a_all[me] = pack_mine(attn).astype(BF16)
        to_all(0, a_all)
    with scope('chipd'):
        chip_sum(1, dsend, dpre, drecv)

    with scope('waitd'):
        d_a = unpack(image_sum(1, dpre, drecv))
    with scope('vjp'):
        inner = jnp.sum(d_a * attn, axis=1, keepdims=True)
        d_s = attn * (d_a - inner)
        d_cos = temp * d_s
        d_t = jnp.sum(jnp.sum(d_s * cosine, axis=1, keepdims=True), axis=0, keepdims=True)
        e_all[me] = pack_mine(d_cos / den).astype(BF16)
        ec = d_cos * cosine
        dsq_c = -0.5 * jnp.sum(ec, axis=1, keepdims=True) / sq_c
        dsk_r = -0.5 * jnp.sum(ec, axis=0, keepdims=True) / sk_r
        st_all[me, 0:1, :] = jnp.sum(jnp.where(diag, dsq_c, 0.0), axis=0, keepdims=True)
        st_all[me, 1:2, :] = dsk_r
        st_all[me, 2:3, :] = jnp.broadcast_to(d_t, (1, 2 * hd))
        to_all(1, e_all)
        to_all(2, st_all)

    def fill(bd, blocks):
        for h in range(heads):
            g, hh = h // hpg, h % hpg
            p = blocks[h].astype(F32)
            rolled = pltpu.roll(p, hd, axis=1)
            mine = (lane32 < hd) if h % 2 == 0 else (lane32 >= hd)
            top, bot = (p, rolled) if h % 2 == 0 else (rolled, p)
            c = slice((hh // 2) * 128, (hh // 2) * 128 + 128)
            bd[g, hh * hd:hh * hd + hd // 2, c] = jnp.where(mine, top, 0.0).astype(BF16)
            bd[g, hh * hd + hd // 2:hh * hd + hd, c] = jnp.where(mine, bot, 0.0).astype(BF16)

    hr = gw.shape[3] // 2
    lo, hi = slice(0, hr), slice(hr, 2 * hr)
    npc = gw.shape[0]

    def put_rows(pc, c, val, sem):
        gw[pc, c] = val.reshape(gw.shape[2:])
        remote(gw.at[pc, c, 1 - core], pre.at[pc, c], pre_s.at[0], pre_r.at[sem], partner)().start()

    def put(pc, val):
        gw[pc] = val.reshape(gw.shape[1:])
        remote(gw.at[pc, :, 1 - core], pre.at[pc], pre_s.at[0], pre_r.at[pc], partner)().start()

    def add_rows(pc, c):
        pre[pc, c] = pre[pc, c] + gw[pc, c, core]

    def send_far(pc):
        add_rows(pc, c_o)
        remote(pre.at[pc, c_o, lo], opp.at[pc, 0], opp_s.at[0], opp_r.at[pc], right)().start()
        remote(pre.at[pc, c_o, hi], opp.at[pc, 1], opp_s.at[0], opp_r.at[pc], left)().start()

    def send_near(pc):
        add_rows(pc, c_r)
        remote(pre.at[pc, c_r, hi], fin.at[pc, 0], fin_s.at[0], fin_r.at[pc], right)().start()
        add_rows(pc, c_l)
        remote(pre.at[pc, c_l, lo], fin.at[pc, 1], fin_s.at[0], fin_r.at[pc], left)().start()
        add_rows(pc, chip)

    def rs_first(pc):
        with scope('first%d' % pc):
            wait_bytes(pre.at[pc], pre_r.at[pc])
            send_far(pc)
            send_near(pc)

    def rs_relay(pc):
        with scope('relay%d' % pc):
            wait_bytes(opp.at[pc], opp_r.at[pc])
            pre[pc, c_r, lo] = pre[pc, c_r, lo] + opp[pc, 0]
            remote(pre.at[pc, c_r, lo], fin.at[pc, 2], fin_s.at[0], fin_r.at[pc], right)().start()
            pre[pc, c_l, hi] = pre[pc, c_l, hi] + opp[pc, 1]
            remote(pre.at[pc, c_l, hi], fin.at[pc, 3], fin_s.at[0], fin_r.at[pc], left)().start()

    def rs_final(pc):
        with scope('final%d' % pc):
            wait_bytes(fin.at[pc], fin_r.at[pc])
            gwst[pc, lo] = pre[pc, chip, lo] + fin[pc, 2] + fin[pc, 1]
            gwst[pc, hi] = pre[pc, chip, hi] + fin[pc, 0] + fin[pc, 3]

    def c3(i):
        t = tile_of(i)
        for g in range(ngrp):
            o_v[t, cols(g)] = mm(v_v[t, cols(g)], bd_a[g], NT).astype(BF16)

    def c4(i):
        t = tile_of(i)
        for g in range(ngrp):
            dqkv_v[t, 2 * width + 256 * g:2 * width + 256 * g + 256] = mm(do_v[t, cols(g)], bd_a[g]).astype(BF16)

    with scope('waita'):
        from_all(0, a_all)
    with scope('c3'):
        fill(bd_a, a_all)
        for i in range(nt):
            c3(i)
    rows_of = 2 * gw.shape[3]

    def gw_rows(c):
        return mm(o_v[:, pl.ds(pl.multiple_of(c * rows_of, rows_of), rows_of)], dy_v[...], TN)

    with scope('gw0a'):
        put_rows(0, c_o, gw_rows(c_o), 0)
    with scope('gw0b'):
        for c in (c_r, c_l, chip):
            put_rows(0, c, gw_rows(c), npc)
    with scope('far0'):
        wait_bytes(pre.at[0, 0], pre_r.at[0])
        send_far(0)

    with scope('c4'):
        for i in range(nt):
            c4(i)
    with scope('near0'):
        wait_bytes(pre.at[0, 1:nchip], pre_r.at[npc])
        send_near(0)

    def gw_piece(p, c):
        with scope('gw%d' % p):
            put(p, mm(u_v[...], dqkv_v[:, c * width:(c + 1) * width], TN))

    gw_piece(1, 2)

    with scope('waite'):
        from_all(1, e_all)
        from_all(2, st_all)
    with scope('fillg'):
        fill(bd_g, e_all)
        pair = [st_all[2 * j, 0:2, :] + st_all[2 * j + 1, 0:2, :] for j in range(heads // 2)]
        dsq2 = jnp.concatenate([2.0 * p[0:1] for p in pair], axis=1)
        dsk2 = jnp.concatenate([2.0 * p[1:2] for p in pair], axis=1)
        lane1 = lax.broadcasted_iota(jnp.int32, (1, 2 * hd), 1)
        gt = jnp.zeros((1, 2 * hd), F32)
        for h in range(heads):
            gt = jnp.where(lane1 == h, st_all[h, 2:3, :], gt)
        gtemp_ref[...] = gt[:, 0:heads]

    def c5(i):
        t = tile_of(i)
        for g in range(ngrp):
            c = cols(g)
            dqkv_v[t, c] = (mm(k_v[t, c], bd_g[g], NT) + q_v[t, c].astype(F32) * dsq2[:, c]).astype(BF16)

    def c6(i):
        t = tile_of(i)
        for g in range(ngrp):
            c = cols(g)
            dqkv_v[t, width + 256 * g:width + 256 * g + 256] = (
                mm(q_v[t, c], bd_g[g]) + k_v[t, c].astype(F32) * dsk2[:, c]).astype(BF16)

    with scope('c5a'):
        for i in range(nt // 2):
            c5(i)
    rs_relay(0)
    with scope('c5b'):
        for i in range(nt // 2, nt):
            c5(i)
    gw_piece(2, 0)
    rs_first(1)
    with scope('c6'):
        for i in range(nt):
            c6(i)
    gw_piece(3, 1)
    rs_first(2)

    def c7(i):
        t = tile_of(i)
        out_v[t, :] = (x_v[t, :].astype(F32) + mm(o_v[t, :], wout_v[...])).astype(BF16)

    def c8(i):
        t = tile_of(i)
        du = mm(dqkv_v[t, :], wqkv_v[...], NT)
        rstd = rstd_v[t, :]
        xhat = (x_v[t, :].astype(F32) - mean_v[t, :]) * rstd
        p = du * xhat
        accumulate(gbacc, 0, jnp.sum(p.reshape(tile // 8, 8, width), axis=0), i == 0)
        accumulate(gbacc, 1, jnp.sum(du.reshape(tile // 8, 8, width), axis=0), i == 0)
        dxh = du * gain_v[...]
        m1 = jnp.mean(dxh, axis=1, keepdims=True)
        m2 = jnp.mean(p * gain_v[...], axis=1, keepdims=True)
        dx = rstd * (dxh - m1 - xhat * m2)
        gtok_v[t, :] = (dy_v[t, :].astype(F32) + dx).astype(BF16)

    with scope('c8a'):
        c8(0)
    rs_relay(1)
    rs_first(3)
    with scope('c8b'):
        c8(1)
    with scope('c8c'):
        c8(2)
    rs_relay(2)
    with scope('c8d'):
        c8(3)
        for n in range(2):
            row_sum = jnp.sum(gbacc[n], axis=0, keepdims=True)
            for j in range(width // 128):
                gb_all[me, 4 * n + j:4 * n + j + 1, :] = row_sum[:, 128 * j:128 * j + 128]
        to_all(3, gb_all)
    with scope('c7a'):
        for i in range(nt // 2):
            c7(i)
    rs_relay(3)
    with scope('c7b'):
        for i in range(nt // 2, nt):
            c7(i)
    for pc in range(npc):
        rs_final(pc)

    with scope('gb'):
        from_all(3, gb_all)
        gb = gb_all[0]
        for d in range(1, ns):
            gb = gb + gb_all[d]
        for j in range(width // 128):
            ggain_ref[:, 128 * j:128 * j + 128] = gb[j:j + 1]
            gbias_ref[:, 128 * j:128 * j + 128] = gb[4 + j:5 + j]

    with scope('drain'):
        for kind, mid in enumerate((gpre, dpre)):
            wait_bytes(mid, own_s.at[kind, 0])
            wait_bytes(mid.at[1:nchip], own_s.at[kind, 1])
        for kind, buf in enumerate((a_all, e_all, st_all, gb_all)):
            wait_bytes(buf.at[0:ns - 1], all_s.at[kind])
        wait_bytes(pre, pre_s.at[0])
        wait_bytes(opp, opp_s.at[0])
        wait_bytes(fin, fin_s.at[0])


def writer(width, out_v, gtok_v, gwst, gg_v, gb_v, gt_v, out_hbm, gtok_hbm, gwqkv_hbm, gwout_hbm, gg_hbm, gb_hbm, gt_hbm, sem):
    copies = [(out_v, out_hbm), (gtok_v, gtok_hbm), (gg_v, gg_hbm), (gb_v, gb_hbm), (gt_v, gt_hbm), (gwst.at[0], gwout_hbm)]
    copies += [(gwst.at[pc], gwqkv_hbm.at[:, pl.ds(c * width, width)]) for pc, c in ((1, 2), (2, 0), (3, 1))]
    for i, (src, dst) in enumerate(copies):
        pltpu.make_async_copy(src, dst, sem.at[i]).start()
    for i, (src, dst) in enumerate(copies):
        pltpu.make_async_copy(src, dst, sem.at[i]).wait()


def solution(mesh):
    ns = mesh.shape['sp']
    row_spec = P(('dp', 'sp'), None)
    part_spec = P('dp')

    def local_step(x, dy, gain, bias, w_qkv, w_out, temp):
        rows, width = x.shape
        heads = temp.shape[0]
        hd = width // heads
        tile = 512
        nt = rows // tile
        share = width // ns
        nchip = ns // 2
        ngrp = width // 256
        hbm = pl.BlockSpec(memory_space=pl.ANY)
        vmem = pl.BlockSpec(memory_space=pltpu.VMEM)
        tok = lambda: pltpu.VMEM((rows, width), BF16)
        outs = pl.pallas_call(
            functools.partial(kernel, ns, rows, width, heads, tile),
            out_shape=[pltpu.VMEM((rows, width), BF16), pltpu.VMEM((rows, width), BF16),
                       pltpu.VMEM((4, share, width), F32), pltpu.VMEM((1, width), F32),
                       pltpu.VMEM((1, width), F32), pltpu.VMEM((1, heads), F32)],
            in_specs=[hbm] * 6 + [pl.BlockSpec(memory_space=pltpu.SMEM)],
            out_specs=[vmem] * 6,
            scratch_shapes=[
                tok(), tok(), pltpu.VMEM((1, width), F32), pltpu.VMEM((1, width), F32),
                pltpu.VMEM((width, 3 * width), BF16), pltpu.VMEM((width, width), BF16),
                tok(), tok(), tok(), tok(), tok(), tok(), pltpu.VMEM((rows, 3 * width), BF16),
                pltpu.VMEM((rows, 1), F32), pltpu.VMEM((rows, 1), F32),
                pltpu.VMEM((ngrp, 256, 256), F32), pltpu.VMEM((ngrp, 256, 256), F32),
                pltpu.VMEM((8, width), F32), pltpu.VMEM((8, width), F32),
                pltpu.VMEM((nchip, 2, hd // 2 + 8, 2 * hd), F32), pltpu.VMEM((nchip, hd // 2 + 8, 2 * hd), F32),
                pltpu.VMEM((nchip, hd // 2 + 8, 2 * hd), F32),
                pltpu.VMEM((nchip, 2, hd // 2, 2 * hd), F32), pltpu.VMEM((nchip, hd // 2, 2 * hd), F32),
                pltpu.VMEM((nchip, hd // 2, 2 * hd), F32),
                pltpu.VMEM((heads, hd // 2, 2 * hd), BF16), pltpu.VMEM((heads, hd // 2, 2 * hd), BF16),
                pltpu.VMEM((heads, 8, 2 * hd), F32),
                pltpu.VMEM((ngrp, 256, 256), BF16), pltpu.VMEM((ngrp, 256, 256), BF16),
                pltpu.VMEM((4, nchip, 2, share, width), F32), pltpu.VMEM((4, nchip, share, width), F32),
                pltpu.VMEM((4, 2, share // 2, width), F32), pltpu.VMEM((4, 4, share // 2, width), F32),
                pltpu.VMEM((2, 8, width), F32), pltpu.VMEM((ns, 8, 128), F32),
                pltpu.SemaphoreType.DMA((nt + 6,)),
                pltpu.SemaphoreType.DMA((2, 2)), pltpu.SemaphoreType.DMA((2, 2)),
                pltpu.SemaphoreType.DMA((4,)), pltpu.SemaphoreType.DMA((4,)),
                pltpu.SemaphoreType.DMA((1,)), pltpu.SemaphoreType.DMA((5,)),
                pltpu.SemaphoreType.DMA((1,)), pltpu.SemaphoreType.DMA((4,)),
                pltpu.SemaphoreType.DMA((1,)), pltpu.SemaphoreType.DMA((4,)),
            ],
            compiler_params=pltpu.CompilerParams(collective_id=0, has_side_effects=True,
                                                 vmem_limit_bytes=52 * 1024 * 1024),
        )(x, dy, gain.reshape(1, -1), bias.reshape(1, -1), w_qkv, w_out, temp)
        out, gtok, gwqkv, gwout, ggain, gbias, gtemp = pl.pallas_call(
            functools.partial(writer, width),
            out_shape=[jax.ShapeDtypeStruct((rows, width), BF16),
                       jax.ShapeDtypeStruct((rows, width), BF16),
                       jax.ShapeDtypeStruct((share, 3 * width), F32),
                       jax.ShapeDtypeStruct((share, width), F32),
                       jax.ShapeDtypeStruct((1, width), F32),
                       jax.ShapeDtypeStruct((1, width), F32),
                       jax.ShapeDtypeStruct((1, heads), F32)],
            in_specs=[vmem] * 6,
            out_specs=[hbm] * 7,
            scratch_shapes=[pltpu.SemaphoreType.DMA((9,))],
            compiler_params=pltpu.CompilerParams(vmem_limit_bytes=1024 * 1024),
        )(*outs)
        return out, gtok, gwqkv, gwout, ggain.reshape(-1), gbias.reshape(-1), gtemp.reshape(-1)

    full = P()
    return jax.shard_map(local_step, mesh=mesh,
                         in_specs=(row_spec, row_spec, full, full, full, full, full),
                         out_specs=(row_spec, row_spec, row_spec, row_spec, part_spec, part_spec, part_spec),
                         check_vma=False)
```

time: 218 us -> 45.3 us (0.21)
  waiting for transfers between devices: 79 us -> 0 us
  matrix products: 63.5 us -> 0 us
  Pallas kernels: 0 us -> 44.4 us
  blocking collectives: 29.9 us -> 0 us
  other arithmetic: 25.5 us -> 0 us
  between operations: 14.1 us -> 0.8 us
  local copies, waits for them, and re-layouts: 5.38 us -> 0 us
    psum x2 -> x0, waiting for transfers between devices: 74.7 us -> none  [the longest x1 40.9 us: local_step(): d_probs = lax.psum(probs_part, 'sp')]
    dot_general x14 -> x0, matrix products: 63.5 us -> none  [the longest x2 10.2 us: apply_attn(): jnp.einsum('nhj,hij->nhi', v_heads, attn_weights, preferred_element_type=...]
    pallas_call x0 -> x2, Pallas kernels: none -> 44.4 us  [the longest x1 42.2 us: local_step(): pl.pallas_call(functools.partial(kernel, ns, rows, width, heads, tile), o...]
    psum x2 -> x0, blocking collectives: 29.9 us -> none  [the longest x1 16.1 us: local_step(): gram_sum, q_sq, k_sq = lax.psum((gram_part, qsq_part, ksq_part), 'sp')]
    reduce_sum x7 -> x0, other arithmetic: 13.3 us -> none  [the longest x2 4.96 us: layer_norm(): row_var = jnp.mean(centered * centered, axis=-1, keepdims=True)]
    unnamed x30 -> x0, local copies, waits for them, and re-layouts: 5.35 us -> none
    convert_element_type x1 -> x0, other arithmetic: 5.26 us -> none  [local_step(): grad_tokens = (dy_loc.astype(jnp.float32) + d_x).astype(jnp.bfloat16)]
    sub x2 -> x0, other arithmetic: 4.15 us -> none  [attn_probs(): return jax.nn.softmax(value_a11[..., None, None] * cosine, axis=-1)]
  transfers between devices with their start and end apart: 4 -> 0, of which waited for: 3 -> 0; matrix products, arithmetic and copies ran while one was open for 27% -> 0% of each run, Pallas kernels for 0% -> 0%
where the time goes in v3:
time: 45.3 us; the launch traced here: 45.2 us
  Pallas kernels  44.4 us (98%)
  between operations  0.8 us (2%)
    pallas_call x1, Pallas kernels, local_step(): pl.pallas_call(functools.partial(kernel, ns, rows, width, heads, tile), o...  42.2 us
    pallas_call x1, Pallas kernels, local_step(): pl.pallas_call(functools.partial(writer, width), out_shape=[jax.ShapeDtyp...  2.25 us

profile of v3, /device:TPU:112, one launch (start us, length us, event | category | flops | bytes accessed | tf_op | source)
XLA Modules:
  0.0 45.2 jit_solution(12261067973231378078)
XLA Ops:
  0.6 42.2 %shard_map.126 = (bf16[2048,512]{1,0:T(8,128)(2,1)S(1)}, bf16[2048,512]{1,0:T(8,128)(2,1)S(1)}, f32[4,64,512]{2,1,0:T(8,128)S(1)}, f32[1,512]{1,0:T(1,128)S(1)},...) custom-call(bf16[2048,512]{1,0:T(8,128)(2,1)} %x_hbm.1, bf16[2048,512]{1,0:T(8,128)(2,1)} %dy_hbm.1, f32[1,512]{1,0:T(1,128)} %bitcast.5, ...), custom_call_target="tpu_custom_call" | custom-call | tf_op jit(solution)/shard_map/pallas_call | solution.py:507
  42.8 2.2 %shard_map.127 = (bf16[2048,512]{1,0:T(8,128)(2,1)}, bf16[2048,512]{1,0:T(8,128)(2,1)}, f32[64,1536]{1,0:T(8,128)}, f32[64,512]{1,0:T(8,128)}, f32[1,512]{1,0:T(...) custom-call(bf16[2048,512]{1,0:T(8,128)(2,1)S(1)} %get-tuple-element.20.out_v, bf16[2048,512]{1,0:T(8,128)(2,1)S(1)} %get-tuple-element.21.gtok_v, ...), custom_call_target="tpu_custom_call" | custom-call | tf_op jit(solution)/shard_map/pallas_call | solution.py:541

commit v4 on v3

--- a/solution.py
+++ b/solution.py
@@ -20,10 +20,10 @@
 
 
 def kernel(ns, rows, width, heads, tile,
-           x_hbm, dy_hbm, gain_hbm, bias_hbm, wqkv_hbm, wout_hbm, temp_ref,
+           x_hbm, dy_hbm, gain_hbm, bias_hbm, wqkv_hbm, wout_hbm, temp_hbm,
            out_v, gtok_v, gwst, ggain_ref, gbias_ref, gtemp_ref,
-           x_v, dy_v, gain_v, bias_v, wqkv_v, wout_v,
-           u_v, q_v, k_v, v_v, do_v, o_v, dqkv_v, mean_v, rstd_v,
+           x_v, dy_v, gain_v, bias_v, wqkv_v, wout_v, temp_ref,
+           u_v, q_v, k_v, v_v, do_v, ut_v, vt_v, ot_v, dqkv_v, mean_v, rstd_v,
            gacc, dacc, sqacc, skacc, gsend, gpre, grecv, dsend, dpre, drecv, a_all, e_all, st_all, bd_a, bd_g,
            gw, pre, opp, fin, gbacc, gb_all,
            in_sem, own_s, own_r, all_s, all_r, pre_s, pre_r, opp_s, opp_r, fin_s, fin_r):
@@ -52,9 +52,6 @@
     peers = [2 * lax.rem(chip + s, nchip) + c for s in far_first for c in (core, 1 - core)] + [partner]
 
     barrier = pltpu.get_barrier_semaphore()
-    for dev in peers:
-        pl.semaphore_signal(barrier, inc=1, device_id={'sp': dev}, device_id_type=pl.DeviceIdType.MESH)
-
     def ld(i, src, dst):
         return lambda: pltpu.make_async_copy(src, dst, in_sem.at[i])
 
@@ -70,21 +67,18 @@
     wqk_copy = ld(nt + 3, wqkv_hbm.at[:, 0:2 * width], wqkv_v.at[:, 0:2 * width])
     wv_copy = ld(nt + 4, wqkv_hbm.at[:, 2 * width:3 * width], wqkv_v.at[:, 2 * width:3 * width])
     wout_copy = ld(nt + 5, wout_hbm, wout_v)
+    temp_copy = ld(nt + 6, temp_hbm, temp_ref)
+    x_copy(0)().start()
     gain_copy().start()
     bias_copy().start()
-    x_copy(0)().start()
     wqk_copy().start()
-    for i in range(1, nt):
-        x_copy(i)().start()
-    wv_copy().start()
-    wout_copy().start()
-    dy_copy().start()
+    x_copy(1)().start()
+    for dev in peers:
+        pl.semaphore_signal(barrier, inc=1, device_id={'sp': dev}, device_id_type=pl.DeviceIdType.MESH)
 
     with scope('init'):
         bd_a[...] = jnp.zeros_like(bd_a)
         bd_g[...] = jnp.zeros_like(bd_g)
-        gain_copy().wait()
-        bias_copy().wait()
 
     ngrp = width // 256
     hpg = heads // ngrp
@@ -113,33 +107,38 @@
         part = jnp.sum((v32 * v32).reshape(tile // 8, 8, 256), axis=0)
         ref[:, c] = part if first else ref[:, c] + part
 
-    nsub = 2 * ngrp
-    sub = tile // nsub
-
-    def ln_sub(i, j):
-        if i < nt:
-            ln(slice(i * tile + j * sub, i * tile + (j + 1) * sub))
-
+    with scope('wx0'):
+        x_copy(0)().wait()
+        for i in range(2, nt):
+            x_copy(i)().start()
+        gain_copy().wait()
+        bias_copy().wait()
+    with scope('ln0'):
+        ln(tile_of(0))
+    with scope('ww'):
+        wqk_copy().wait()
+        x_copy(1)().wait()
+        wv_copy().start()
+        wout_copy().start()
+        dy_copy().start()
+        temp_copy().start()
     with scope('c1'):
-        x_copy(0)().wait()
-        for j in range(nsub):
-            ln_sub(0, j)
-        wqk_copy().wait()
-        for i in range(1, nt):
-            x_copy(i)().wait()
         for i in range(nt):
             t = tile_of(i)
+            if i == 1:
+                for j in range(2, nt):
+                    x_copy(j)().wait()
+            if i + 1 < nt:
+                ln(tile_of(i + 1))
+            q = mm(u_v[t, :], wqkv_v[:, 0:width]).astype(BF16)
+            q_v[t, :] = q
+            k = mm(u_v[t, :], wqkv_v[:, width:2 * width]).astype(BF16)
+            k_v[t, :] = k
             for g in range(ngrp):
                 c = cols(g)
-                q = mm(u_v[t, :], wqkv_v[:, c]).astype(BF16)
-                q_v[t, c] = q
-                square_sum(sqacc, c, q, i == 0)
-                ln_sub(i + 1, 2 * g)
-                k = mm(u_v[t, :], wqkv_v[:, width + 256 * g:width + 256 * g + 256]).astype(BF16)
-                k_v[t, c] = k
-                square_sum(skacc, c, k, i == 0)
-                ln_sub(i + 1, 2 * g + 1)
-                accumulate(gacc, g, mm(q, k, TN), i == 0)
+                square_sum(sqacc, c, q[:, c], i == 0)
+                square_sum(skacc, c, k[:, c], i == 0)
+                accumulate(gacc, g, mm(q[:, c], k[:, c], TN), i == 0)
 
     lane32 = lax.broadcasted_iota(jnp.int32, (hd // 2, 2 * hd), 1)
 
@@ -245,6 +244,7 @@
         sq_c = jnp.sum(jnp.where(diag, sq_r, 0.0), axis=1, keepdims=True)
         den = jnp.sqrt(sq_c) * jnp.sqrt(sk_r)
         cosine = gram / den
+        temp_copy().wait()
         temp = temp_ref[me]
         logits = jnp.where(half, temp * cosine, -jnp.inf)
         ex = jnp.exp(logits - jnp.max(logits, axis=1, keepdims=True))
@@ -254,22 +254,23 @@
     with scope('chipd'):
         chip_sum(1, dsend, dpre, drecv)
 
-    with scope('waitd'):
-        d_a = unpack(image_sum(1, dpre, drecv))
-    with scope('vjp'):
-        inner = jnp.sum(d_a * attn, axis=1, keepdims=True)
-        d_s = attn * (d_a - inner)
-        d_cos = temp * d_s
-        d_t = jnp.sum(jnp.sum(d_s * cosine, axis=1, keepdims=True), axis=0, keepdims=True)
-        e_all[me] = pack_mine(d_cos / den).astype(BF16)
-        ec = d_cos * cosine
-        dsq_c = -0.5 * jnp.sum(ec, axis=1, keepdims=True) / sq_c
-        dsk_r = -0.5 * jnp.sum(ec, axis=0, keepdims=True) / sk_r
-        st_all[me, 0:1, :] = jnp.sum(jnp.where(diag, dsq_c, 0.0), axis=0, keepdims=True)
-        st_all[me, 1:2, :] = dsk_r
-        st_all[me, 2:3, :] = jnp.broadcast_to(d_t, (1, 2 * hd))
-        to_all(1, e_all)
-        to_all(2, st_all)
+    def head_vjp():
+        with scope('waitd'):
+            d_a = unpack(image_sum(1, dpre, drecv))
+        with scope('vjp'):
+            inner = jnp.sum(d_a * attn, axis=1, keepdims=True)
+            d_s = attn * (d_a - inner)
+            d_cos = temp * d_s
+            d_t = jnp.sum(jnp.sum(d_s * cosine, axis=1, keepdims=True), axis=0, keepdims=True)
+            e_all[me] = pack_mine(d_cos / den).astype(BF16)
+            ec = d_cos * cosine
+            dsq_c = -0.5 * jnp.sum(ec, axis=1, keepdims=True) / sq_c
+            dsk_r = -0.5 * jnp.sum(ec, axis=0, keepdims=True) / sk_r
+            st_all[me, 0:1, :] = jnp.sum(jnp.where(diag, dsq_c, 0.0), axis=0, keepdims=True)
+            st_all[me, 1:2, :] = dsk_r
+            st_all[me, 2:3, :] = jnp.broadcast_to(d_t, (1, 2 * hd))
+            to_all(1, e_all)
+            to_all(2, st_all)
 
     def fill(bd, blocks):
         for h in range(heads):
@@ -286,34 +287,34 @@
     lo, hi = slice(0, hr), slice(hr, 2 * hr)
     npc = gw.shape[0]
 
-    def put_rows(pc, c, val, sem):
-        gw[pc, c] = val.reshape(gw.shape[2:])
-        remote(gw.at[pc, c, 1 - core], pre.at[pc, c], pre_s.at[0], pre_r.at[sem], partner)().start()
-
-    def put(pc, val):
-        gw[pc] = val.reshape(gw.shape[1:])
-        remote(gw.at[pc, :, 1 - core], pre.at[pc], pre_s.at[0], pre_r.at[pc], partner)().start()
-
-    def add_rows(pc, c):
+    nhalf = nchip // 2
+    half_rows = nhalf * 2 * gw.shape[3]
+    near_half = lax.rem(c_o // nhalf + 1, 2)
+    far_half = 1 - near_half
+
+    def put(pc, n, lhs, rhs):
+        first = (far_half, near_half)[n]
+        val = mm(lhs[pl.ds(pl.multiple_of(first * half_rows, half_rows), half_rows), :], rhs)
+        c = pl.ds(first * nhalf, nhalf)
+        gw[pc, c] = val.reshape(nhalf, *gw.shape[2:])
+        remote(gw.at[pc, c, 1 - core], pre.at[pc, c], pre_s.at[0], pre_r.at[pc, n], partner)().start()
+
+    def add_half(pc, n):
+        wait_bytes(pre.at[pc, 0:nhalf], pre_r.at[pc, n])
+        c = pl.ds((far_half, near_half)[n] * nhalf, nhalf)
         pre[pc, c] = pre[pc, c] + gw[pc, c, core]
 
-    def send_far(pc):
-        add_rows(pc, c_o)
-        remote(pre.at[pc, c_o, lo], opp.at[pc, 0], opp_s.at[0], opp_r.at[pc], right)().start()
-        remote(pre.at[pc, c_o, hi], opp.at[pc, 1], opp_s.at[0], opp_r.at[pc], left)().start()
-
-    def send_near(pc):
-        add_rows(pc, c_r)
-        remote(pre.at[pc, c_r, hi], fin.at[pc, 0], fin_s.at[0], fin_r.at[pc], right)().start()
-        add_rows(pc, c_l)
-        remote(pre.at[pc, c_l, lo], fin.at[pc, 1], fin_s.at[0], fin_r.at[pc], left)().start()
-        add_rows(pc, chip)
-
-    def rs_first(pc):
-        with scope('first%d' % pc):
-            wait_bytes(pre.at[pc], pre_r.at[pc])
-            send_far(pc)
-            send_near(pc)
+    def rs_far(pc):
+        with scope('far%d' % pc):
+            add_half(pc, 0)
+            remote(pre.at[pc, c_o, lo], opp.at[pc, 0], opp_s.at[0], opp_r.at[pc], right)().start()
+            remote(pre.at[pc, c_o, hi], opp.at[pc, 1], opp_s.at[0], opp_r.at[pc], left)().start()
+
+    def rs_near(pc):
+        with scope('near%d' % pc):
+            add_half(pc, 1)
+            remote(pre.at[pc, c_r, hi], fin.at[pc, 0], fin_s.at[0], fin_r.at[pc], right)().start()
+            remote(pre.at[pc, c_l, lo], fin.at[pc, 1], fin_s.at[0], fin_r.at[pc], left)().start()
 
     def rs_relay(pc):
         with scope('relay%d' % pc):
@@ -329,48 +330,59 @@
             gwst[pc, lo] = pre[pc, chip, lo] + fin[pc, 2] + fin[pc, 1]
             gwst[pc, hi] = pre[pc, chip, hi] + fin[pc, 0] + fin[pc, 3]
 
-    def c3(i):
-        t = tile_of(i)
-        for g in range(ngrp):
-            o_v[t, cols(g)] = mm(v_v[t, cols(g)], bd_a[g], NT).astype(BF16)
+    def c3(g):
+        with scope('c3'):
+            c = pl.ds(pl.multiple_of(g * 256, 256), 256)
+            for i in range(nt):
+                t = tile_of(i)
+                ot_v[c, t] = mm(bd_a[g], vt_v[c, t]).astype(BF16)
 
     def c4(i):
         t = tile_of(i)
         for g in range(ngrp):
             dqkv_v[t, 2 * width + 256 * g:2 * width + 256 * g + 256] = mm(do_v[t, cols(g)], bd_a[g]).astype(BF16)
 
+    with scope('transpose'):
+        for i in range(nt):
+            t = tile_of(i)
+            ut_v[:, t] = u_v[t, :].T
+            vt_v[:, t] = v_v[t, :].T
     with scope('waita'):
         from_all(0, a_all)
-    with scope('c3'):
+    with scope('filla'):
         fill(bd_a, a_all)
-        for i in range(nt):
-            c3(i)
-    rows_of = 2 * gw.shape[3]
-
-    def gw_rows(c):
-        return mm(o_v[:, pl.ds(pl.multiple_of(c * rows_of, rows_of), rows_of)], dy_v[...], TN)
-
-    with scope('gw0a'):
-        put_rows(0, c_o, gw_rows(c_o), 0)
-    with scope('gw0b'):
-        for c in (c_r, c_l, chip):
-            put_rows(0, c, gw_rows(c), npc)
-    with scope('far0'):
-        wait_bytes(pre.at[0, 0], pre_r.at[0])
-        send_far(0)
+    def gw_piece(pc, n, lhs, rhs):
+        with scope('gw%d%s' % (pc, 'ab'[n])):
+            put(pc, n, lhs, rhs)
+
+    def dcols(c):
+        return dqkv_v[:, c * width:(c + 1) * width]
+
+    def c7(i):
+        t = tile_of(i)
+        out_v[t, :] = (x_v[t, :].astype(F32) + mm(ot_v[:, t], wout_v[...], TN)).astype(BF16)
+
+    c3(far_half)
+    gw_piece(0, 0, ot_v, dy_v[...])
+    c3(near_half)
+    gw_piece(0, 1, ot_v, dy_v[...])
+    head_vjp()
+    rs_far(0)
 
     with scope('c4'):
         for i in range(nt):
             c4(i)
-    with scope('near0'):
-        wait_bytes(pre.at[0, 1:nchip], pre_r.at[npc])
-        send_near(0)
-
-    def gw_piece(p, c):
-        with scope('gw%d' % p):
-            put(p, mm(u_v[...], dqkv_v[:, c * width:(c + 1) * width], TN))
-
-    gw_piece(1, 2)
+    rs_near(0)
+    gw_piece(1, 0, ut_v, dcols(2))
+    gw_piece(1, 1, ut_v, dcols(2))
+    with scope('c7a'):
+        for i in range(nt // 2):
+            c7(i)
+    rs_far(1)
+    with scope('c7b'):
+        for i in range(nt // 2, nt):
+            c7(i)
+    rs_near(1)
 
     with scope('waite'):
         from_all(1, e_all)
@@ -399,24 +411,20 @@
             dqkv_v[t, width + 256 * g:width + 256 * g + 256] = (
                 mm(q_v[t, c], bd_g[g]) + k_v[t, c].astype(F32) * dsk2[:, c]).astype(BF16)
 
-    with scope('c5a'):
-        for i in range(nt // 2):
+    with scope('c5'):
+        for i in range(nt):
             c5(i)
     rs_relay(0)
-    with scope('c5b'):
-        for i in range(nt // 2, nt):
-            c5(i)
-    gw_piece(2, 0)
-    rs_first(1)
+    gw_piece(2, 0, ut_v, dcols(0))
+    gw_piece(2, 1, ut_v, dcols(0))
     with scope('c6'):
         for i in range(nt):
             c6(i)
-    gw_piece(3, 1)
-    rs_first(2)
-
-    def c7(i):
-        t = tile_of(i)
-        out_v[t, :] = (x_v[t, :].astype(F32) + mm(o_v[t, :], wout_v[...])).astype(BF16)
+    rs_far(2)
+    gw_piece(3, 0, ut_v, dcols(1))
+    rs_near(2)
+    gw_piece(3, 1, ut_v, dcols(1))
+    rs_relay(1)
 
     def c8(i):
         t = tile_of(i)
@@ -434,13 +442,13 @@
 
     with scope('c8a'):
         c8(0)
-    rs_relay(1)
-    rs_first(3)
+    rs_far(3)
+    rs_near(3)
     with scope('c8b'):
         c8(1)
+    rs_relay(2)
     with scope('c8c'):
         c8(2)
-    rs_relay(2)
     with scope('c8d'):
         c8(3)
         for n in range(2):
@@ -448,13 +456,7 @@
             for j in range(width // 128):
                 gb_all[me, 4 * n + j:4 * n + j + 1, :] = row_sum[:, 128 * j:128 * j + 128]
         to_all(3, gb_all)
-    with scope('c7a'):
-        for i in range(nt // 2):
-            c7(i)
     rs_relay(3)
-    with scope('c7b'):
-        for i in range(nt // 2, nt):
-            c7(i)
     for pc in range(npc):
         rs_final(pc)
 
@@ -479,8 +481,9 @@
 
 
 def writer(width, out_v, gtok_v, gwst, gg_v, gb_v, gt_v, out_hbm, gtok_hbm, gwqkv_hbm, gwout_hbm, gg_hbm, gb_hbm, gt_hbm, sem):
-    copies = [(out_v, out_hbm), (gtok_v, gtok_hbm), (gg_v, gg_hbm), (gb_v, gb_hbm), (gt_v, gt_hbm), (gwst.at[0], gwout_hbm)]
+    copies = [(gg_v, gg_hbm), (gb_v, gb_hbm), (gt_v, gt_hbm), (gwst.at[0], gwout_hbm)]
     copies += [(gwst.at[pc], gwqkv_hbm.at[:, pl.ds(c * width, width)]) for pc, c in ((1, 2), (2, 0), (3, 1))]
+    copies += [(out_v, out_hbm), (gtok_v, gtok_hbm)]
     for i, (src, dst) in enumerate(copies):
         pltpu.make_async_copy(src, dst, sem.at[i]).start()
     for i, (src, dst) in enumerate(copies):
@@ -504,17 +507,18 @@
         hbm = pl.BlockSpec(memory_space=pl.ANY)
         vmem = pl.BlockSpec(memory_space=pltpu.VMEM)
         tok = lambda: pltpu.VMEM((rows, width), BF16)
+        tok_t = lambda: pltpu.VMEM((width, rows), BF16)
         outs = pl.pallas_call(
             functools.partial(kernel, ns, rows, width, heads, tile),
             out_shape=[pltpu.VMEM((rows, width), BF16), pltpu.VMEM((rows, width), BF16),
                        pltpu.VMEM((4, share, width), F32), pltpu.VMEM((1, width), F32),
                        pltpu.VMEM((1, width), F32), pltpu.VMEM((1, heads), F32)],
-            in_specs=[hbm] * 6 + [pl.BlockSpec(memory_space=pltpu.SMEM)],
+            in_specs=[hbm] * 7,
             out_specs=[vmem] * 6,
             scratch_shapes=[
                 tok(), tok(), pltpu.VMEM((1, width), F32), pltpu.VMEM((1, width), F32),
-                pltpu.VMEM((width, 3 * width), BF16), pltpu.VMEM((width, width), BF16),
-                tok(), tok(), tok(), tok(), tok(), tok(), pltpu.VMEM((rows, 3 * width), BF16),
+                pltpu.VMEM((width, 3 * width), BF16), pltpu.VMEM((width, width), BF16), pltpu.SMEM((heads,), F32),
+                tok(), tok(), tok(), tok(), tok(), tok_t(), tok_t(), tok_t(), pltpu.VMEM((rows, 3 * width), BF16),
                 pltpu.VMEM((rows, 1), F32), pltpu.VMEM((rows, 1), F32),
                 pltpu.VMEM((ngrp, 256, 256), F32), pltpu.VMEM((ngrp, 256, 256), F32),
                 pltpu.VMEM((8, width), F32), pltpu.VMEM((8, width), F32),
@@ -528,10 +532,10 @@
                 pltpu.VMEM((4, nchip, 2, share, width), F32), pltpu.VMEM((4, nchip, share, width), F32),
                 pltpu.VMEM((4, 2, share // 2, width), F32), pltpu.VMEM((4, 4, share // 2, width), F32),
                 pltpu.VMEM((2, 8, width), F32), pltpu.VMEM((ns, 8, 128), F32),
-                pltpu.SemaphoreType.DMA((nt + 6,)),
+                pltpu.SemaphoreType.DMA((nt + 7,)),
                 pltpu.SemaphoreType.DMA((2, 2)), pltpu.SemaphoreType.DMA((2, 2)),
                 pltpu.SemaphoreType.DMA((4,)), pltpu.SemaphoreType.DMA((4,)),
-                pltpu.SemaphoreType.DMA((1,)), pltpu.SemaphoreType.DMA((5,)),
+                pltpu.SemaphoreType.DMA((1,)), pltpu.SemaphoreType.DMA((4, 2)),
                 pltpu.SemaphoreType.DMA((1,)), pltpu.SemaphoreType.DMA((4,)),
                 pltpu.SemaphoreType.DMA((1,)), pltpu.SemaphoreType.DMA((4,)),
             ],

time: 45.3 us -> 43.1 us (0.951)
  Pallas kernels: 44.4 us -> 42.1 us
    pallas_call x1, Pallas kernels: 42.2 us -> 39.8 us  [local_step(): pl.pallas_call(functools.partial(kernel, ns, rows, width, heads, tile), o...]
where the time goes in v4:
time: 43.1 us; the launch traced here: 42.9 us
  Pallas kernels  42.1 us (98%)
  between operations  0.8 us (2%)
    pallas_call x1, Pallas kernels, local_step(): pl.pallas_call(functools.partial(kernel, ns, rows, width, heads, tile), o...  39.8 us
    pallas_call x1, Pallas kernels, local_step(): pl.pallas_call(functools.partial(writer, width), out_shape=[jax.ShapeDtyp...  2.27 us

profile of v4, /device:TPU:112, one launch (start us, length us, event | category | flops | bytes accessed | tf_op | source)
XLA Modules:
  0.0 42.9 jit_solution(7879728341339959004)
XLA Ops:
  0.6 39.8 %shard_map.126 = (bf16[2048,512]{1,0:T(8,128)(2,1)S(1)}, bf16[2048,512]{1,0:T(8,128)(2,1)S(1)}, f32[4,64,512]{2,1,0:T(8,128)S(1)}, f32[1,512]{1,0:T(1,128)S(1)},...) custom-call(bf16[2048,512]{1,0:T(8,128)(2,1)} %x_hbm.1, bf16[2048,512]{1,0:T(8,128)(2,1)} %dy_hbm.1, f32[1,512]{1,0:T(1,128)} %bitcast.5, ...), custom_call_target="tpu_custom_call" | custom-call | tf_op jit(solution)/shard_map/pallas_call | solution.py:511
  40.5 2.3 %shard_map.127 = (bf16[2048,512]{1,0:T(8,128)(2,1)}, bf16[2048,512]{1,0:T(8,128)(2,1)}, f32[64,1536]{1,0:T(8,128)}, f32[64,512]{1,0:T(8,128)}, f32[1,512]{1,0:T(...) custom-call(bf16[2048,512]{1,0:T(8,128)(2,1)S(1)} %get-tuple-element.20.out_v, bf16[2048,512]{1,0:T(8,128)(2,1)S(1)} %get-tuple-element.21.gtok_v, ...), custom_call_target="tpu_custom_call" | custom-call | tf_op jit(solution)/shard_map/pallas_call | solution.py:545

commit v5 on v4

--- a/solution.py
+++ b/solution.py
@@ -64,14 +64,21 @@
     dy_copy = ld(nt, dy_hbm, dy_v)
     gain_copy = ld(nt + 1, gain_hbm, gain_v)
     bias_copy = ld(nt + 2, bias_hbm, bias_v)
-    wqk_copy = ld(nt + 3, wqkv_hbm.at[:, 0:2 * width], wqkv_v.at[:, 0:2 * width])
+    wq_copy = ld(nt + 3, wqkv_hbm.at[:, 0:width], wqkv_v.at[:, 0:width])
+    wk_copy = ld(nt + 7, wqkv_hbm.at[:, width:2 * width], wqkv_v.at[:, width:2 * width])
     wv_copy = ld(nt + 4, wqkv_hbm.at[:, 2 * width:3 * width], wqkv_v.at[:, 2 * width:3 * width])
     wout_copy = ld(nt + 5, wout_hbm, wout_v)
     temp_copy = ld(nt + 6, temp_hbm, temp_ref)
-    x_copy(0)().start()
+    head = slice(0, tile // 2)
+    rest = slice(tile // 2, tile)
+    x_head = ld(0, x_hbm.at[head], x_v.at[head])
+    x_rest = ld(nt + 8, x_hbm.at[rest], x_v.at[rest])
+    x_head().start()
     gain_copy().start()
     bias_copy().start()
-    wqk_copy().start()
+    wq_copy().start()
+    x_rest().start()
+    wk_copy().start()
     x_copy(1)().start()
     for dev in peers:
         pl.semaphore_signal(barrier, inc=1, device_id={'sp': dev}, device_id_type=pl.DeviceIdType.MESH)
@@ -108,15 +115,21 @@
         ref[:, c] = part if first else ref[:, c] + part
 
     with scope('wx0'):
-        x_copy(0)().wait()
+        x_head().wait()
         for i in range(2, nt):
             x_copy(i)().start()
         gain_copy().wait()
         bias_copy().wait()
     with scope('ln0'):
-        ln(tile_of(0))
+        ln(head)
     with scope('ww'):
-        wqk_copy().wait()
+        wq_copy().wait()
+        x_rest().wait()
+    with scope('c1h'):
+        ln(rest)
+        q_v[head, :] = mm(u_v[head, :], wqkv_v[:, 0:width]).astype(BF16)
+    with scope('ww2'):
+        wk_copy().wait()
         x_copy(1)().wait()
         wv_copy().start()
         wout_copy().start()
@@ -130,8 +143,12 @@
                     x_copy(j)().wait()
             if i + 1 < nt:
                 ln(tile_of(i + 1))
-            q = mm(u_v[t, :], wqkv_v[:, 0:width]).astype(BF16)
-            q_v[t, :] = q
+            if i == 0:
+                q_v[rest, :] = mm(u_v[rest, :], wqkv_v[:, 0:width]).astype(BF16)
+                q = q_v[t, :]
+            else:
+                q = mm(u_v[t, :], wqkv_v[:, 0:width]).astype(BF16)
+                q_v[t, :] = q
             k = mm(u_v[t, :], wqkv_v[:, width:2 * width]).astype(BF16)
             k_v[t, :] = k
             for g in range(ngrp):
@@ -194,25 +211,24 @@
         pl.semaphore_wait(barrier, ns - 1)
         to_partner(0, gsend, gpre)().start()
 
-    def c2(i):
-        t = tile_of(i)
-        v = mm(u_v[t, :], wqkv_v[:, 2 * width:3 * width]).astype(BF16)
-        v_v[t, :] = v
-        do = mm(dy_v[t, :], wout_v[...], NT).astype(BF16)
-        do_v[t, :] = do
-        for g in range(ngrp):
-            accumulate(dacc, g, mm(do[:, cols(g)], v[:, cols(g)], TN), i == 0)
-
+    def v_rows(t):
+        v_v[t, :] = mm(u_v[t, :], wqkv_v[:, 2 * width:3 * width]).astype(BF16)
+
+    cut = rows - tile
     with scope('c2a'):
         wv_copy().wait()
-        wout_copy().wait()
-        dy_copy().wait()
-        c2(0)
+        v_rows(slice(0, cut))
     with scope('chipg'):
         chip_sum(0, gsend, gpre, grecv)
     with scope('c2b'):
-        for i in range(1, nt):
-            c2(i)
+        wout_copy().wait()
+        dy_copy().wait()
+        v_rows(slice(cut, rows))
+        for i in range(nt):
+            t = tile_of(i)
+            do_v[t, :] = mm(dy_v[t, :], wout_v[...], NT).astype(BF16)
+        for g in range(ngrp):
+            dacc[g] = mm(do_v[:, cols(g)], v_v[:, cols(g)], TN)
     with scope('sendd'):
         for h in range(heads):
             dsend[h // 2, h % 2] = pack(dacc, h)
@@ -254,23 +270,21 @@
     with scope('chipd'):
         chip_sum(1, dsend, dpre, drecv)
 
-    def head_vjp():
-        with scope('waitd'):
-            d_a = unpack(image_sum(1, dpre, drecv))
-        with scope('vjp'):
-            inner = jnp.sum(d_a * attn, axis=1, keepdims=True)
-            d_s = attn * (d_a - inner)
-            d_cos = temp * d_s
-            d_t = jnp.sum(jnp.sum(d_s * cosine, axis=1, keepdims=True), axis=0, keepdims=True)
-            e_all[me] = pack_mine(d_cos / den).astype(BF16)
-            ec = d_cos * cosine
-            dsq_c = -0.5 * jnp.sum(ec, axis=1, keepdims=True) / sq_c
-            dsk_r = -0.5 * jnp.sum(ec, axis=0, keepdims=True) / sk_r
-            st_all[me, 0:1, :] = jnp.sum(jnp.where(diag, dsq_c, 0.0), axis=0, keepdims=True)
-            st_all[me, 1:2, :] = dsk_r
-            st_all[me, 2:3, :] = jnp.broadcast_to(d_t, (1, 2 * hd))
-            to_all(1, e_all)
-            to_all(2, st_all)
+    def vjp_gram():
+        d_a = unpack(image_sum(1, dpre, drecv))
+        inner = jnp.sum(d_a * attn, axis=1, keepdims=True)
+        d_s = attn * (d_a - inner)
+        d_cos = temp * d_s
+        e_all[me] = pack_mine(d_cos / den).astype(BF16)
+        return d_s, d_cos * cosine
+
+    def vjp_rest(d_s, ec):
+        d_t = jnp.sum(jnp.sum(d_s * cosine, axis=1, keepdims=True), axis=0, keepdims=True)
+        dsq_c = -0.5 * jnp.sum(ec, axis=1, keepdims=True) / sq_c
+        dsk_r = -0.5 * jnp.sum(ec, axis=0, keepdims=True) / sk_r
+        st_all[me, 0:1, :] = jnp.sum(jnp.where(diag, dsq_c, 0.0), axis=0, keepdims=True)
+        st_all[me, 1:2, :] = dsk_r
+        st_all[me, 2:3, :] = jnp.broadcast_to(d_t, (1, 2 * hd))
 
     def fill(bd, blocks):
         for h in range(heads):
@@ -333,9 +347,7 @@
     def c3(g):
         with scope('c3'):
             c = pl.ds(pl.multiple_of(g * 256, 256), 256)
-            for i in range(nt):
-                t = tile_of(i)
-                ot_v[c, t] = mm(bd_a[g], vt_v[c, t]).astype(BF16)
+            ot_v[c, :] = mm(bd_a[g], vt_v[c, :]).astype(BF16)
 
     def c4(i):
         t = tile_of(i)
@@ -363,26 +375,25 @@
         out_v[t, :] = (x_v[t, :].astype(F32) + mm(ot_v[:, t], wout_v[...], TN)).astype(BF16)
 
     c3(far_half)
-    gw_piece(0, 0, ot_v, dy_v[...])
+    with scope('gw0a'):
+        vjp_rest(*vjp_gram())
+        put(0, 0, ot_v, dy_v[...])
+        to_all(1, e_all)
+        to_all(2, st_all)
     c3(near_half)
     gw_piece(0, 1, ot_v, dy_v[...])
-    head_vjp()
     rs_far(0)
 
     with scope('c4'):
         for i in range(nt):
             c4(i)
+    gw_piece(1, 0, ut_v, dcols(2))
     rs_near(0)
-    gw_piece(1, 0, ut_v, dcols(2))
     gw_piece(1, 1, ut_v, dcols(2))
     with scope('c7a'):
         for i in range(nt // 2):
             c7(i)
     rs_far(1)
-    with scope('c7b'):
-        for i in range(nt // 2, nt):
-            c7(i)
-    rs_near(1)
 
     with scope('waite'):
         from_all(1, e_all)
@@ -414,18 +425,19 @@
     with scope('c5'):
         for i in range(nt):
             c5(i)
+    rs_near(1)
+    gw_piece(2, 0, ut_v, dcols(0))
     rs_relay(0)
-    gw_piece(2, 0, ut_v, dcols(0))
-    gw_piece(2, 1, ut_v, dcols(0))
     with scope('c6'):
         for i in range(nt):
             c6(i)
+    gw_piece(3, 0, ut_v, dcols(1))
     rs_far(2)
-    gw_piece(3, 0, ut_v, dcols(1))
-    rs_near(2)
+    gw_piece(2, 1, ut_v, dcols(0))
+    rs_far(3)
     gw_piece(3, 1, ut_v, dcols(1))
     rs_relay(1)
-
+    rs_near(2)
     def c8(i):
         t = tile_of(i)
         du = mm(dqkv_v[t, :], wqkv_v[...], NT)
@@ -442,13 +454,12 @@
 
     with scope('c8a'):
         c8(0)
-    rs_far(3)
     rs_near(3)
     with scope('c8b'):
         c8(1)
-    rs_relay(2)
     with scope('c8c'):
         c8(2)
+    rs_relay(2)
     with scope('c8d'):
         c8(3)
         for n in range(2):
@@ -457,6 +468,9 @@
                 gb_all[me, 4 * n + j:4 * n + j + 1, :] = row_sum[:, 128 * j:128 * j + 128]
         to_all(3, gb_all)
     rs_relay(3)
+    with scope('c7b'):
+        for i in range(nt // 2, nt):
+            c7(i)
     for pc in range(npc):
         rs_final(pc)
 
@@ -532,7 +546,7 @@
                 pltpu.VMEM((4, nchip, 2, share, width), F32), pltpu.VMEM((4, nchip, share, width), F32),
                 pltpu.VMEM((4, 2, share // 2, width), F32), pltpu.VMEM((4, 4, share // 2, width), F32),
                 pltpu.VMEM((2, 8, width), F32), pltpu.VMEM((ns, 8, 128), F32),
-                pltpu.SemaphoreType.DMA((nt + 7,)),
+                pltpu.SemaphoreType.DMA((nt + 9,)),
                 pltpu.SemaphoreType.DMA((2, 2)), pltpu.SemaphoreType.DMA((2, 2)),
                 pltpu.SemaphoreType.DMA((4,)), pltpu.SemaphoreType.DMA((4,)),
                 pltpu.SemaphoreType.DMA((1,)), pltpu.SemaphoreType.DMA((4, 2)),

time: 43.1 us -> 42.1 us (0.977)
  Pallas kernels: 42.1 us -> 41.2 us
    pallas_call x1, Pallas kernels: 39.8 us -> 38.9 us  [local_step(): pl.pallas_call(functools.partial(kernel, ns, rows, width, heads, tile), o...]
where the time goes in v5:
time: 42.1 us; the launch traced here: 42 us
  Pallas kernels  41.2 us (98%)
  between operations  0.8 us (2%)
    pallas_call x1, Pallas kernels, local_step(): pl.pallas_call(functools.partial(kernel, ns, rows, width, heads, tile), o...  38.9 us
    pallas_call x1, Pallas kernels, local_step(): pl.pallas_call(functools.partial(writer, width), out_shape=[jax.ShapeDtyp...  2.27 us

profile of v5, /device:TPU:112, one launch (start us, length us, event | category | flops | bytes accessed | tf_op | source)
XLA Modules:
  0.0 42.0 jit_solution(3177187346964106183)
XLA Ops:
  0.6 38.9 %shard_map.126 = (bf16[2048,512]{1,0:T(8,128)(2,1)S(1)}, bf16[2048,512]{1,0:T(8,128)(2,1)S(1)}, f32[4,64,512]{2,1,0:T(8,128)S(1)}, f32[1,512]{1,0:T(1,128)S(1)},...) custom-call(bf16[2048,512]{1,0:T(8,128)(2,1)} %x_hbm.1, bf16[2048,512]{1,0:T(8,128)(2,1)} %dy_hbm.1, f32[1,512]{1,0:T(1,128)} %bitcast.5, ...), custom_call_target="tpu_custom_call" | custom-call | tf_op jit(solution)/shard_map/pallas_call | solution.py:525
  39.5 2.3 %shard_map.127 = (bf16[2048,512]{1,0:T(8,128)(2,1)}, bf16[2048,512]{1,0:T(8,128)(2,1)}, f32[64,1536]{1,0:T(8,128)}, f32[64,512]{1,0:T(8,128)}, f32[1,512]{1,0:T(...) custom-call(bf16[2048,512]{1,0:T(8,128)(2,1)S(1)} %get-tuple-element.20.out_v, bf16[2048,512]{1,0:T(8,128)(2,1)S(1)} %get-tuple-element.21.gtok_v, ...), custom_call_target="tpu_custom_call" | custom-call | tf_op jit(solution)/shard_map/pallas_call | solution.py:559

commit v6 on v5

--- a/solution.py
+++ b/solution.py
@@ -155,7 +155,11 @@
                 c = cols(g)
                 square_sum(sqacc, c, q[:, c], i == 0)
                 square_sum(skacc, c, k[:, c], i == 0)
-                accumulate(gacc, g, mm(q[:, c], k[:, c], TN), i == 0)
+                if i == nt - 2:
+                    done = slice(0, (nt - 1) * tile)
+                    gacc[g] = mm(q_v[done, c], k_v[done, c], TN)
+                elif i == nt - 1:
+                    gacc[g] += mm(q[:, c], k[:, c], TN)
 
     lane32 = lax.broadcasted_iota(jnp.int32, (hd // 2, 2 * hd), 1)
 
@@ -214,7 +218,7 @@
     def v_rows(t):
         v_v[t, :] = mm(u_v[t, :], wqkv_v[:, 2 * width:3 * width]).astype(BF16)
 
-    cut = rows - tile
+    cut = rows // 2
     with scope('c2a'):
         wv_copy().wait()
         v_rows(slice(0, cut))
@@ -432,10 +436,23 @@
         for i in range(nt):
             c6(i)
     gw_piece(3, 0, ut_v, dcols(1))
-    rs_far(2)
+    @pl.when(core == 0)
+    def _():
+        rs_far(2)
+
     gw_piece(2, 1, ut_v, dcols(0))
-    rs_far(3)
+
+    @pl.when(core == 0)
+    def _():
+        rs_far(3)
+
     gw_piece(3, 1, ut_v, dcols(1))
+
+    @pl.when(core == 1)
+    def _():
+        rs_far(2)
+        rs_far(3)
+
     rs_relay(1)
     rs_near(2)
     def c8(i):

time: 42.1 us -> 41.9 us (level); the launches traced: 42 us -> 41.3 us
  Pallas kernels: 41.2 us -> 40.5 us
    pallas_call x1, Pallas kernels: 38.9 us -> 38.2 us  [local_step(): pl.pallas_call(functools.partial(kernel, ns, rows, width, heads, tile), o...]
where the time goes in v6:
time: 41.9 us; the launch traced here: 41.3 us
  Pallas kernels  40.5 us (97%)
  between operations  0.8 us (2%)
    pallas_call x1, Pallas kernels, local_step(): pl.pallas_call(functools.partial(kernel, ns, rows, width, heads, tile), o...  38.2 us
    pallas_call x1, Pallas kernels, local_step(): pl.pallas_call(functools.partial(writer, width), out_shape=[jax.ShapeDtyp...  2.27 us

profile of v6, /device:TPU:112, one launch (start us, length us, event | category | flops | bytes accessed | tf_op | source)
XLA Modules:
  0.0 41.3 jit_solution(6395585110102757512)
XLA Ops:
  0.6 38.2 %shard_map.126 = (bf16[2048,512]{1,0:T(8,128)(2,1)S(1)}, bf16[2048,512]{1,0:T(8,128)(2,1)S(1)}, f32[4,64,512]{2,1,0:T(8,128)S(1)}, f32[1,512]{1,0:T(1,128)S(1)},...) custom-call(bf16[2048,512]{1,0:T(8,128)(2,1)} %x_hbm.1, bf16[2048,512]{1,0:T(8,128)(2,1)} %dy_hbm.1, f32[1,512]{1,0:T(1,128)} %bitcast.5, ...), custom_call_target="tpu_custom_call" | custom-call | tf_op jit(solution)/shard_map/pallas_call | solution.py:542
  38.8 2.3 %shard_map.127 = (bf16[2048,512]{1,0:T(8,128)(2,1)}, bf16[2048,512]{1,0:T(8,128)(2,1)}, f32[64,1536]{1,0:T(8,128)}, f32[64,512]{1,0:T(8,128)}, f32[1,512]{1,0:T(...) custom-call(bf16[2048,512]{1,0:T(8,128)(2,1)S(1)} %get-tuple-element.20.out_v, bf16[2048,512]{1,0:T(8,128)(2,1)S(1)} %get-tuple-element.21.gtok_v, ...), custom_call_target="tpu_custom_call" | custom-call | tf_op jit(solution)/shard_map/pallas_call | solution.py:576

commit v7 on v6

--- a/solution.py
+++ b/solution.py
@@ -25,7 +25,7 @@
            x_v, dy_v, gain_v, bias_v, wqkv_v, wout_v, temp_ref,
            u_v, q_v, k_v, v_v, do_v, ut_v, vt_v, ot_v, dqkv_v, mean_v, rstd_v,
            gacc, dacc, sqacc, skacc, gsend, gpre, grecv, dsend, dpre, drecv, a_all, e_all, st_all, bd_a, bd_g,
-           gw, pre, opp, fin, gbacc, gb_all,
+           gw, pre, opp, fin, gbacc, gb_mine, gb_mate, gb_all,
            in_sem, own_s, own_r, all_s, all_r, pre_s, pre_r, opp_s, opp_r, fin_s, fin_r):
     me = lax.axis_index('sp')
     nt = rows // tile
@@ -49,7 +49,7 @@
         pltpu.make_async_copy(ref, ref, sem).wait()
 
     far_first = sorted(range(1, nchip), key=lambda s: -min(s, nchip - s))
-    peers = [2 * lax.rem(chip + s, nchip) + c for s in far_first for c in (core, 1 - core)] + [partner]
+    peers = [2 * lax.rem(chip + s, nchip) + c for s in far_first for c in (1, 0)] + [partner]
 
     barrier = pltpu.get_barrier_semaphore()
     def ld(i, src, dst):
@@ -194,11 +194,11 @@
             mid[c, 0:n] = mid[c, 0:n] + src[c, core, 0:n]
         for s in far_first:
             c = lax.rem(chip + s, nchip)
-            remote(mid.at[c], dst.at[s], own_s.at[kind, 1], own_r.at[kind, 1], 2 * c + core)().start()
+            remote(mid.at[c, 0:n], dst.at[s, 0:n], own_s.at[kind, 1], own_r.at[kind, 1], 2 * c + core)().start()
 
     def image_sum(kind, mid, dst):
         n = mid.shape[1] if kind else hd // 2 + 2
-        wait_bytes(dst.at[1:nchip], own_r.at[kind, 1])
+        wait_bytes(dst.at[1:nchip, 0:n], own_r.at[kind, 1])
         tot = mid[chip, 0:n]
         for s in range(1, nchip):
             tot = tot + dst[s, 0:n]
@@ -383,7 +383,9 @@
         vjp_rest(*vjp_gram())
         put(0, 0, ot_v, dy_v[...])
         to_all(1, e_all)
-        to_all(2, st_all)
+        for dev in peers:
+            st = st_all.at[me, 0:3]
+            remote(st, st, all_s.at[2], all_r.at[2], dev)().start()
     c3(near_half)
     gw_piece(0, 1, ot_v, dy_v[...])
     rs_far(0)
@@ -401,7 +403,7 @@
 
     with scope('waite'):
         from_all(1, e_all)
-        from_all(2, st_all)
+        wait_bytes(st_all.at[0:ns - 1, 0:3], all_r.at[2])
     with scope('fillg'):
         fill(bd_g, e_all)
         pair = [st_all[2 * j, 0:2, :] + st_all[2 * j + 1, 0:2, :] for j in range(heads // 2)]
@@ -482,19 +484,24 @@
         for n in range(2):
             row_sum = jnp.sum(gbacc[n], axis=0, keepdims=True)
             for j in range(width // 128):
-                gb_all[me, 4 * n + j:4 * n + j + 1, :] = row_sum[:, 128 * j:128 * j + 128]
-        to_all(3, gb_all)
+                gb_mine[4 * n + j:4 * n + j + 1, :] = row_sum[:, 128 * j:128 * j + 128]
+        remote(gb_mine, gb_mate, own_s.at[2, 0], own_r.at[2, 0], partner)().start()
     rs_relay(3)
     with scope('c7b'):
         for i in range(nt // 2, nt):
             c7(i)
+    with scope('gbchip'):
+        wait_bytes(gb_mate, own_r.at[2, 0])
+        gb_all[chip] = gb_mine[...] + gb_mate[...]
+        for n in far_first:
+            remote(gb_all.at[chip], gb_all.at[chip], own_s.at[2, 1], own_r.at[2, 1], 2 * lax.rem(chip + n, nchip) + core)().start()
     for pc in range(npc):
         rs_final(pc)
 
     with scope('gb'):
-        from_all(3, gb_all)
+        wait_bytes(gb_all.at[1:nchip], own_r.at[2, 1])
         gb = gb_all[0]
-        for d in range(1, ns):
+        for d in range(1, nchip):
             gb = gb + gb_all[d]
         for j in range(width // 128):
             ggain_ref[:, 128 * j:128 * j + 128] = gb[j:j + 1]
@@ -503,9 +510,12 @@
     with scope('drain'):
         for kind, mid in enumerate((gpre, dpre)):
             wait_bytes(mid, own_s.at[kind, 0])
-            wait_bytes(mid.at[1:nchip], own_s.at[kind, 1])
-        for kind, buf in enumerate((a_all, e_all, st_all, gb_all)):
+            wait_bytes(mid.at[1:nchip, 0:mid.shape[1] if kind else hd // 2 + 2], own_s.at[kind, 1])
+        wait_bytes(gb_mate, own_s.at[2, 0])
+        wait_bytes(gb_all.at[1:nchip], own_s.at[2, 1])
+        for kind, buf in enumerate((a_all, e_all)):
             wait_bytes(buf.at[0:ns - 1], all_s.at[kind])
+        wait_bytes(st_all.at[0:ns - 1, 0:3], all_s.at[2])
         wait_bytes(pre, pre_s.at[0])
         wait_bytes(opp, opp_s.at[0])
         wait_bytes(fin, fin_s.at[0])
@@ -562,10 +572,10 @@
                 pltpu.VMEM((ngrp, 256, 256), BF16), pltpu.VMEM((ngrp, 256, 256), BF16),
                 pltpu.VMEM((4, nchip, 2, share, width), F32), pltpu.VMEM((4, nchip, share, width), F32),
                 pltpu.VMEM((4, 2, share // 2, width), F32), pltpu.VMEM((4, 4, share // 2, width), F32),
-                pltpu.VMEM((2, 8, width), F32), pltpu.VMEM((ns, 8, 128), F32),
+                pltpu.VMEM((2, 8, width), F32), pltpu.VMEM((8, 128), F32), pltpu.VMEM((8, 128), F32), pltpu.VMEM((nchip, 8, 128), F32),
                 pltpu.SemaphoreType.DMA((nt + 9,)),
-                pltpu.SemaphoreType.DMA((2, 2)), pltpu.SemaphoreType.DMA((2, 2)),
-                pltpu.SemaphoreType.DMA((4,)), pltpu.SemaphoreType.DMA((4,)),
+                pltpu.SemaphoreType.DMA((3, 2)), pltpu.SemaphoreType.DMA((3, 2)),
+                pltpu.SemaphoreType.DMA((3,)), pltpu.SemaphoreType.DMA((3,)),
                 pltpu.SemaphoreType.DMA((1,)), pltpu.SemaphoreType.DMA((4, 2)),
                 pltpu.SemaphoreType.DMA((1,)), pltpu.SemaphoreType.DMA((4,)),
                 pltpu.SemaphoreType.DMA((1,)), pltpu.SemaphoreType.DMA((4,)),

time: 41.9 us -> 41.7 us (level)
  no operation moved by 1% of the time
where the time goes in v7:
time: 41.7 us; the launch traced here: 41.1 us
  Pallas kernels  40.3 us (97%)
  between operations  0.8 us (2%)
    pallas_call x1, Pallas kernels, local_step(): pl.pallas_call(functools.partial(kernel, ns, rows, width, heads, tile), o...  38 us
    pallas_call x1, Pallas kernels, local_step(): pl.pallas_call(functools.partial(writer, width), out_shape=[jax.ShapeDtyp...  2.27 us

profile of v7, /device:TPU:112, one launch (start us, length us, event | category | flops | bytes accessed | tf_op | source)
XLA Modules:
  0.0 41.1 jit_solution(7747641879881686033)
XLA Ops:
  0.6 38.0 %shard_map.126 = (bf16[2048,512]{1,0:T(8,128)(2,1)S(1)}, bf16[2048,512]{1,0:T(8,128)(2,1)S(1)}, f32[4,64,512]{2,1,0:T(8,128)S(1)}, f32[1,512]{1,0:T(1,128)S(1)},...) custom-call(bf16[2048,512]{1,0:T(8,128)(2,1)} %x_hbm.1, bf16[2048,512]{1,0:T(8,128)(2,1)} %dy_hbm.1, f32[1,512]{1,0:T(1,128)} %bitcast.5, ...), custom_call_target="tpu_custom_call" | custom-call | tf_op jit(solution)/shard_map/pallas_call | solution.py:552
  38.6 2.3 %shard_map.127 = (bf16[2048,512]{1,0:T(8,128)(2,1)}, bf16[2048,512]{1,0:T(8,128)(2,1)}, f32[64,1536]{1,0:T(8,128)}, f32[64,512]{1,0:T(8,128)}, f32[1,512]{1,0:T(...) custom-call(bf16[2048,512]{1,0:T(8,128)(2,1)S(1)} %get-tuple-element.20.out_v, bf16[2048,512]{1,0:T(8,128)(2,1)S(1)} %get-tuple-element.21.gtok_v, ...), custom_call_target="tpu_custom_call" | custom-call | tf_op jit(solution)/shard_map/pallas_call | solution.py:586

commit v8 on v7

--- a/solution.py
+++ b/solution.py
@@ -30,6 +30,8 @@
     me = lax.axis_index('sp')
     nt = rows // tile
     hd = width // heads
+    keep = True
+    hf, wide, w2, w3 = hd // 2, 2 * hd, 2 * width, 3 * width
     core = lax.rem(me, 2)
     chip = me // 2
     nchip = ns // 2
@@ -65,8 +67,8 @@
     gain_copy = ld(nt + 1, gain_hbm, gain_v)
     bias_copy = ld(nt + 2, bias_hbm, bias_v)
     wq_copy = ld(nt + 3, wqkv_hbm.at[:, 0:width], wqkv_v.at[:, 0:width])
-    wk_copy = ld(nt + 7, wqkv_hbm.at[:, width:2 * width], wqkv_v.at[:, width:2 * width])
-    wv_copy = ld(nt + 4, wqkv_hbm.at[:, 2 * width:3 * width], wqkv_v.at[:, 2 * width:3 * width])
+    wk_copy = ld(nt + 7, wqkv_hbm.at[:, width:w2], wqkv_v.at[:, width:w2])
+    wv_copy = ld(nt + 4, wqkv_hbm.at[:, w2:w3], wqkv_v.at[:, w2:w3])
     wout_copy = ld(nt + 5, wout_hbm, wout_v)
     temp_copy = ld(nt + 6, temp_hbm, temp_ref)
     head = slice(0, tile // 2)
@@ -95,9 +97,9 @@
 
     def ln(t):
         x = x_v[t, :].astype(F32)
-        mean = jnp.mean(x, axis=1, keepdims=True)
+        mean = jnp.mean(x, axis=1, keepdims=keep)
         cent = x - mean
-        var = jnp.mean(cent * cent, axis=1, keepdims=True)
+        var = jnp.mean(cent * cent, axis=1, keepdims=keep)
         rstd = lax.rsqrt(var + EPS)
         mean_v[t, :] = mean
         rstd_v[t, :] = rstd
@@ -149,7 +151,7 @@
             else:
                 q = mm(u_v[t, :], wqkv_v[:, 0:width]).astype(BF16)
                 q_v[t, :] = q
-            k = mm(u_v[t, :], wqkv_v[:, width:2 * width]).astype(BF16)
+            k = mm(u_v[t, :], wqkv_v[:, width:w2]).astype(BF16)
             k_v[t, :] = k
             for g in range(ngrp):
                 c = cols(g)
@@ -161,10 +163,10 @@
                 elif i == nt - 1:
                     gacc[g] += mm(q[:, c], k[:, c], TN)
 
-    lane32 = lax.broadcasted_iota(jnp.int32, (hd // 2, 2 * hd), 1)
+    lane32 = lax.broadcasted_iota(jnp.int32, (hf, wide), 1)
 
     def pack_block(blk, odd):
-        top, bot = blk[0:hd // 2], blk[hd // 2:hd]
+        top, bot = blk[0:hf], blk[hf:hd]
         if odd:
             top = pltpu.roll(top, hd, axis=1)
         else:
@@ -176,20 +178,20 @@
         return pack_block(acc[g, hh * hd:hh * hd + hd, (hh // 2) * 128:(hh // 2) * 128 + 128], h % 2 == 1)
 
     with scope('packg'):
-        sq_row = jnp.sum(sqacc[...], axis=0, keepdims=True)
-        sk_row = jnp.sum(skacc[...], axis=0, keepdims=True)
+        sq_row = jnp.sum(sqacc[...], axis=0, keepdims=keep)
+        sk_row = jnp.sum(skacc[...], axis=0, keepdims=keep)
         for h in range(heads):
-            gsend[h // 2, h % 2, 0:hd // 2, :] = pack(gacc, h)
+            gsend[h // 2, h % 2, 0:hf, :] = pack(gacc, h)
             c = slice((h // 2) * 128, (h // 2) * 128 + 128)
-            gsend[h // 2, h % 2, hd // 2:hd // 2 + 1, :] = sq_row[:, c]
-            gsend[h // 2, h % 2, hd // 2 + 1:hd // 2 + 2, :] = sk_row[:, c]
+            gsend[h // 2, h % 2, hf:hf + 1, :] = sq_row[:, c]
+            gsend[h // 2, h % 2, hf + 1:hf + 2, :] = sk_row[:, c]
 
     def to_partner(kind, src, dst):
         return remote(src.at[:, 1 - core], dst, own_s.at[kind, 0], own_r.at[kind, 0], partner)
 
     def chip_sum(kind, src, mid, dst):
         wait_bytes(mid, own_r.at[kind, 0])
-        n = mid.shape[1] if kind else hd // 2 + 2
+        n = mid.shape[1] if kind else hf + 2
         for c in range(nchip):
             mid[c, 0:n] = mid[c, 0:n] + src[c, core, 0:n]
         for s in far_first:
@@ -197,7 +199,7 @@
             remote(mid.at[c, 0:n], dst.at[s, 0:n], own_s.at[kind, 1], own_r.at[kind, 1], 2 * c + core)().start()
 
     def image_sum(kind, mid, dst):
-        n = mid.shape[1] if kind else hd // 2 + 2
+        n = mid.shape[1] if kind else hf + 2
         wait_bytes(dst.at[1:nchip, 0:n], own_r.at[kind, 1])
         tot = mid[chip, 0:n]
         for s in range(1, nchip):
@@ -216,7 +218,7 @@
         to_partner(0, gsend, gpre)().start()
 
     def v_rows(t):
-        v_v[t, :] = mm(u_v[t, :], wqkv_v[:, 2 * width:3 * width]).astype(BF16)
+        v_v[t, :] = mm(u_v[t, :], wqkv_v[:, w2:w3]).astype(BF16)
 
     cut = rows // 2
     with scope('c2a'):
@@ -238,8 +240,8 @@
             dsend[h // 2, h % 2] = pack(dacc, h)
         to_partner(1, dsend, dpre)().start()
 
-    row = lax.broadcasted_iota(jnp.int32, (hd, 2 * hd), 0)
-    lanep = lax.broadcasted_iota(jnp.int32, (hd, 2 * hd), 1) - hd * core
+    row = lax.broadcasted_iota(jnp.int32, (hd, wide), 0)
+    lanep = lax.broadcasted_iota(jnp.int32, (hd, wide), 1) - hd * core
     half = (lanep >= 0) & (lanep < hd)
     diag = lanep == row
     half1 = half[0:1]
@@ -253,22 +255,22 @@
     def pack_mine(blk):
         rolled = pltpu.roll(blk, hd, axis=1)
         low, high = jnp.where(even, blk, rolled), jnp.where(even, rolled, blk)
-        return jnp.where(lane32 < hd, low[0:hd // 2], high[hd // 2:hd])
+        return jnp.where(lane32 < hd, low[0:hf], high[hf:hd])
 
     with scope('waitg'):
         tot = image_sum(0, gpre, grecv)
     with scope('soft'):
-        gram = unpack(tot[0:hd // 2])
-        sq_r = tot[hd // 2:hd // 2 + 1]
-        sk_r = jnp.where(half1, tot[hd // 2 + 1:hd // 2 + 2], 1.0)
-        sq_c = jnp.sum(jnp.where(diag, sq_r, 0.0), axis=1, keepdims=True)
+        gram = unpack(tot[0:hf])
+        sq_r = tot[hf:hf + 1]
+        sk_r = jnp.where(half1, tot[hf + 1:hf + 2], 1.0)
+        sq_c = jnp.sum(jnp.where(diag, sq_r, 0.0), axis=1, keepdims=keep)
         den = jnp.sqrt(sq_c) * jnp.sqrt(sk_r)
         cosine = gram / den
         temp_copy().wait()
         temp = temp_ref[me]
         logits = jnp.where(half, temp * cosine, -jnp.inf)
-        ex = jnp.exp(logits - jnp.max(logits, axis=1, keepdims=True))
-        attn = ex / jnp.sum(ex, axis=1, keepdims=True)
+        ex = jnp.exp(logits - jnp.max(logits, axis=1, keepdims=keep))
+        attn = ex / jnp.sum(ex, axis=1, keepdims=keep)
         a_all[me] = pack_mine(attn).astype(BF16)
         to_all(0, a_all)
     with scope('chipd'):
@@ -276,19 +278,19 @@
 
     def vjp_gram():
         d_a = unpack(image_sum(1, dpre, drecv))
-        inner = jnp.sum(d_a * attn, axis=1, keepdims=True)
+        inner = jnp.sum(d_a * attn, axis=1, keepdims=keep)
         d_s = attn * (d_a - inner)
         d_cos = temp * d_s
         e_all[me] = pack_mine(d_cos / den).astype(BF16)
         return d_s, d_cos * cosine
 
     def vjp_rest(d_s, ec):
-        d_t = jnp.sum(jnp.sum(d_s * cosine, axis=1, keepdims=True), axis=0, keepdims=True)
-        dsq_c = -0.5 * jnp.sum(ec, axis=1, keepdims=True) / sq_c
-        dsk_r = -0.5 * jnp.sum(ec, axis=0, keepdims=True) / sk_r
-        st_all[me, 0:1, :] = jnp.sum(jnp.where(diag, dsq_c, 0.0), axis=0, keepdims=True)
+        d_t = jnp.sum(jnp.sum(d_s * cosine, axis=1, keepdims=keep), axis=0, keepdims=keep)
+        dsq_c = -0.5 * jnp.sum(ec, axis=1, keepdims=keep) / sq_c
+        dsk_r = -0.5 * jnp.sum(ec, axis=0, keepdims=keep) / sk_r
+        st_all[me, 0:1, :] = jnp.sum(jnp.where(diag, dsq_c, 0.0), axis=0, keepdims=keep)
         st_all[me, 1:2, :] = dsk_r
-        st_all[me, 2:3, :] = jnp.broadcast_to(d_t, (1, 2 * hd))
+        st_all[me, 2:3, :] = jnp.broadcast_to(d_t, (1, wide))
 
     def fill(bd, blocks):
         for h in range(heads):
@@ -298,8 +300,8 @@
             mine = (lane32 < hd) if h % 2 == 0 else (lane32 >= hd)
             top, bot = (p, rolled) if h % 2 == 0 else (rolled, p)
             c = slice((hh // 2) * 128, (hh // 2) * 128 + 128)
-            bd[g, hh * hd:hh * hd + hd // 2, c] = jnp.where(mine, top, 0.0).astype(BF16)
-            bd[g, hh * hd + hd // 2:hh * hd + hd, c] = jnp.where(mine, bot, 0.0).astype(BF16)
+            bd[g, hh * hd:hh * hd + hf, c] = jnp.where(mine, top, 0.0).astype(BF16)
+            bd[g, hh * hd + hf:hh * hd + hd, c] = jnp.where(mine, bot, 0.0).astype(BF16)
 
     hr = gw.shape[3] // 2
     lo, hi = slice(0, hr), slice(hr, 2 * hr)
@@ -315,7 +317,7 @@
         val = mm(lhs[pl.ds(pl.multiple_of(first * half_rows, half_rows), half_rows), :], rhs)
         c = pl.ds(first * nhalf, nhalf)
         gw[pc, c] = val.reshape(nhalf, *gw.shape[2:])
-        remote(gw.at[pc, c, 1 - core], pre.at[pc, c], pre_s.at[0], pre_r.at[pc, n], partner)().start()
+        remote(gw.at[pc, c, 1 - core], pre.at[pc, c], pre_s, pre_r.at[pc, n], partner)().start()
 
     def add_half(pc, n):
         wait_bytes(pre.at[pc, 0:nhalf], pre_r.at[pc, n])
@@ -325,22 +327,22 @@
     def rs_far(pc):
         with scope('far%d' % pc):
             add_half(pc, 0)
-            remote(pre.at[pc, c_o, lo], opp.at[pc, 0], opp_s.at[0], opp_r.at[pc], right)().start()
-            remote(pre.at[pc, c_o, hi], opp.at[pc, 1], opp_s.at[0], opp_r.at[pc], left)().start()
+            remote(pre.at[pc, c_o, lo], opp.at[pc, 0], opp_s, opp_r.at[pc], right)().start()
+            remote(pre.at[pc, c_o, hi], opp.at[pc, 1], opp_s, opp_r.at[pc], left)().start()
 
     def rs_near(pc):
         with scope('near%d' % pc):
             add_half(pc, 1)
-            remote(pre.at[pc, c_r, hi], fin.at[pc, 0], fin_s.at[0], fin_r.at[pc], right)().start()
-            remote(pre.at[pc, c_l, lo], fin.at[pc, 1], fin_s.at[0], fin_r.at[pc], left)().start()
+            remote(pre.at[pc, c_r, hi], fin.at[pc, 0], fin_s, fin_r.at[pc], right)().start()
+            remote(pre.at[pc, c_l, lo], fin.at[pc, 1], fin_s, fin_r.at[pc], left)().start()
 
     def rs_relay(pc):
         with scope('relay%d' % pc):
             wait_bytes(opp.at[pc], opp_r.at[pc])
             pre[pc, c_r, lo] = pre[pc, c_r, lo] + opp[pc, 0]
-            remote(pre.at[pc, c_r, lo], fin.at[pc, 2], fin_s.at[0], fin_r.at[pc], right)().start()
+            remote(pre.at[pc, c_r, lo], fin.at[pc, 2], fin_s, fin_r.at[pc], right)().start()
             pre[pc, c_l, hi] = pre[pc, c_l, hi] + opp[pc, 1]
-            remote(pre.at[pc, c_l, hi], fin.at[pc, 3], fin_s.at[0], fin_r.at[pc], left)().start()
+            remote(pre.at[pc, c_l, hi], fin.at[pc, 3], fin_s, fin_r.at[pc], left)().start()
 
     def rs_final(pc):
         with scope('final%d' % pc):
@@ -356,7 +358,7 @@
     def c4(i):
         t = tile_of(i)
         for g in range(ngrp):
-            dqkv_v[t, 2 * width + 256 * g:2 * width + 256 * g + 256] = mm(do_v[t, cols(g)], bd_a[g]).astype(BF16)
+            dqkv_v[t, w2 + 256 * g:w2 + 256 * g + 256] = mm(do_v[t, cols(g)], bd_a[g]).astype(BF16)
 
     with scope('transpose'):
         for i in range(nt):
@@ -409,8 +411,8 @@
         pair = [st_all[2 * j, 0:2, :] + st_all[2 * j + 1, 0:2, :] for j in range(heads // 2)]
         dsq2 = jnp.concatenate([2.0 * p[0:1] for p in pair], axis=1)
         dsk2 = jnp.concatenate([2.0 * p[1:2] for p in pair], axis=1)
-        lane1 = lax.broadcasted_iota(jnp.int32, (1, 2 * hd), 1)
-        gt = jnp.zeros((1, 2 * hd), F32)
+        lane1 = lax.broadcasted_iota(jnp.int32, (1, wide), 1)
+        gt = jnp.zeros((1, wide), F32)
         for h in range(heads):
             gt = jnp.where(lane1 == h, st_all[h, 2:3, :], gt)
         gtemp_ref[...] = gt[:, 0:heads]
@@ -466,8 +468,8 @@
         accumulate(gbacc, 0, jnp.sum(p.reshape(tile // 8, 8, width), axis=0), i == 0)
         accumulate(gbacc, 1, jnp.sum(du.reshape(tile // 8, 8, width), axis=0), i == 0)
         dxh = du * gain_v[...]
-        m1 = jnp.mean(dxh, axis=1, keepdims=True)
-        m2 = jnp.mean(p * gain_v[...], axis=1, keepdims=True)
+        m1 = jnp.mean(dxh, axis=1, keepdims=keep)
+        m2 = jnp.mean(p * gain_v[...], axis=1, keepdims=keep)
         dx = rstd * (dxh - m1 - xhat * m2)
         gtok_v[t, :] = (dy_v[t, :].astype(F32) + dx).astype(BF16)
 
@@ -482,7 +484,7 @@
     with scope('c8d'):
         c8(3)
         for n in range(2):
-            row_sum = jnp.sum(gbacc[n], axis=0, keepdims=True)
+            row_sum = jnp.sum(gbacc[n], axis=0, keepdims=keep)
             for j in range(width // 128):
                 gb_mine[4 * n + j:4 * n + j + 1, :] = row_sum[:, 128 * j:128 * j + 128]
         remote(gb_mine, gb_mate, own_s.at[2, 0], own_r.at[2, 0], partner)().start()
@@ -510,15 +512,15 @@
     with scope('drain'):
         for kind, mid in enumerate((gpre, dpre)):
             wait_bytes(mid, own_s.at[kind, 0])
-            wait_bytes(mid.at[1:nchip, 0:mid.shape[1] if kind else hd // 2 + 2], own_s.at[kind, 1])
+            wait_bytes(mid.at[1:nchip, 0:mid.shape[1] if kind else hf + 2], own_s.at[kind, 1])
         wait_bytes(gb_mate, own_s.at[2, 0])
         wait_bytes(gb_all.at[1:nchip], own_s.at[2, 1])
         for kind, buf in enumerate((a_all, e_all)):
             wait_bytes(buf.at[0:ns - 1], all_s.at[kind])
         wait_bytes(st_all.at[0:ns - 1, 0:3], all_s.at[2])
-        wait_bytes(pre, pre_s.at[0])
-        wait_bytes(opp, opp_s.at[0])
-        wait_bytes(fin, fin_s.at[0])
+        wait_bytes(pre, pre_s)
+        wait_bytes(opp, opp_s)
+        wait_bytes(fin, fin_s)
 
 
 def writer(width, out_v, gtok_v, gwst, gg_v, gb_v, gt_v, out_hbm, gtok_hbm, gwqkv_hbm, gwout_hbm, gg_hbm, gb_hbm, gt_hbm, sem):
@@ -545,6 +547,10 @@
         share = width // ns
         nchip = ns // 2
         ngrp = width // 256
+        hf, wide = hd // 2, 2 * hd
+        f32 = lambda *shape: pltpu.VMEM(shape, F32)
+        b16 = lambda *shape: pltpu.VMEM(shape, BF16)
+        sems = lambda *shape: pltpu.SemaphoreType.DMA(shape)
         hbm = pl.BlockSpec(memory_space=pl.ANY)
         vmem = pl.BlockSpec(memory_space=pltpu.VMEM)
         tok = lambda: pltpu.VMEM((rows, width), BF16)
@@ -557,28 +563,17 @@
             in_specs=[hbm] * 7,
             out_specs=[vmem] * 6,
             scratch_shapes=[
-                tok(), tok(), pltpu.VMEM((1, width), F32), pltpu.VMEM((1, width), F32),
-                pltpu.VMEM((width, 3 * width), BF16), pltpu.VMEM((width, width), BF16), pltpu.SMEM((heads,), F32),
-                tok(), tok(), tok(), tok(), tok(), tok_t(), tok_t(), tok_t(), pltpu.VMEM((rows, 3 * width), BF16),
-                pltpu.VMEM((rows, 1), F32), pltpu.VMEM((rows, 1), F32),
-                pltpu.VMEM((ngrp, 256, 256), F32), pltpu.VMEM((ngrp, 256, 256), F32),
-                pltpu.VMEM((8, width), F32), pltpu.VMEM((8, width), F32),
-                pltpu.VMEM((nchip, 2, hd // 2 + 8, 2 * hd), F32), pltpu.VMEM((nchip, hd // 2 + 8, 2 * hd), F32),
-                pltpu.VMEM((nchip, hd // 2 + 8, 2 * hd), F32),
-                pltpu.VMEM((nchip, 2, hd // 2, 2 * hd), F32), pltpu.VMEM((nchip, hd // 2, 2 * hd), F32),
-                pltpu.VMEM((nchip, hd // 2, 2 * hd), F32),
-                pltpu.VMEM((heads, hd // 2, 2 * hd), BF16), pltpu.VMEM((heads, hd // 2, 2 * hd), BF16),
-                pltpu.VMEM((heads, 8, 2 * hd), F32),
-                pltpu.VMEM((ngrp, 256, 256), BF16), pltpu.VMEM((ngrp, 256, 256), BF16),
-                pltpu.VMEM((4, nchip, 2, share, width), F32), pltpu.VMEM((4, nchip, share, width), F32),
-                pltpu.VMEM((4, 2, share // 2, width), F32), pltpu.VMEM((4, 4, share // 2, width), F32),
-                pltpu.VMEM((2, 8, width), F32), pltpu.VMEM((8, 128), F32), pltpu.VMEM((8, 128), F32), pltpu.VMEM((nchip, 8, 128), F32),
-                pltpu.SemaphoreType.DMA((nt + 9,)),
-                pltpu.SemaphoreType.DMA((3, 2)), pltpu.SemaphoreType.DMA((3, 2)),
-                pltpu.SemaphoreType.DMA((3,)), pltpu.SemaphoreType.DMA((3,)),
-                pltpu.SemaphoreType.DMA((1,)), pltpu.SemaphoreType.DMA((4, 2)),
-                pltpu.SemaphoreType.DMA((1,)), pltpu.SemaphoreType.DMA((4,)),
-                pltpu.SemaphoreType.DMA((1,)), pltpu.SemaphoreType.DMA((4,)),
+                tok(), tok(), f32(1, width), f32(1, width), b16(width, 3 * width), b16(width, width), pltpu.SMEM((heads,), F32),
+                tok(), tok(), tok(), tok(), tok(), tok_t(), tok_t(), tok_t(), b16(rows, 3 * width), f32(rows, 1), f32(rows, 1),
+                f32(ngrp, 256, 256), f32(ngrp, 256, 256), f32(8, width), f32(8, width),
+                f32(nchip, 2, hf + 8, wide), f32(nchip, hf + 8, wide), f32(nchip, hf + 8, wide),
+                f32(nchip, 2, hf, wide), f32(nchip, hf, wide), f32(nchip, hf, wide),
+                b16(heads, hf, wide), b16(heads, hf, wide), f32(heads, 8, wide),
+                b16(ngrp, 256, 256), b16(ngrp, 256, 256),
+                f32(4, nchip, 2, share, width), f32(4, nchip, share, width),
+                f32(4, 2, share // 2, width), f32(4, 4, share // 2, width),
+                f32(2, 8, width), f32(8, 128), f32(8, 128), f32(nchip, 8, 128),
+                sems(nt + 9), sems(3, 2), sems(3, 2), sems(3), sems(3), sems(), sems(4, 2), sems(), sems(4), sems(), sems(4),
             ],
             compiler_params=pltpu.CompilerParams(collective_id=0, has_side_effects=True,
                                                  vmem_limit_bytes=52 * 1024 * 1024),

time: 41.7 us -> 41.7 us (level)
  no operation moved by 1% of the time
where the time goes in v8:
time: 41.7 us; the launch traced here: 41.1 us
  Pallas kernels  40.3 us (97%)
  between operations  0.8 us (2%)
    pallas_call x1, Pallas kernels, local_step(): pl.pallas_call(functools.partial(kernel, ns, rows, width, heads, tile), o...  38 us
    pallas_call x1, Pallas kernels, local_step(): pl.pallas_call(functools.partial(writer, width), out_shape=[jax.ShapeDtyp...  2.27 us

profile of v8, /device:TPU:112, one launch (start us, length us, event | category | flops | bytes accessed | tf_op | source)
XLA Modules:
  0.0 41.1 jit_solution(7747641879881686033)
XLA Ops:
  0.6 38.0 %shard_map.126 = (bf16[2048,512]{1,0:T(8,128)(2,1)S(1)}, bf16[2048,512]{1,0:T(8,128)(2,1)S(1)}, f32[4,64,512]{2,1,0:T(8,128)S(1)}, f32[1,512]{1,0:T(1,128)S(1)},...) custom-call(bf16[2048,512]{1,0:T(8,128)(2,1)} %x_hbm.1, bf16[2048,512]{1,0:T(8,128)(2,1)} %dy_hbm.1, f32[1,512]{1,0:T(1,128)} %bitcast.5, ...), custom_call_target="tpu_custom_call" | custom-call | tf_op jit(solution)/shard_map/pallas_call | solution.py:558
  38.6 2.3 %shard_map.127 = (bf16[2048,512]{1,0:T(8,128)(2,1)}, bf16[2048,512]{1,0:T(8,128)(2,1)}, f32[64,1536]{1,0:T(8,128)}, f32[64,512]{1,0:T(8,128)}, f32[1,512]{1,0:T(...) custom-call(bf16[2048,512]{1,0:T(8,128)(2,1)S(1)} %get-tuple-element.20.out_v, bf16[2048,512]{1,0:T(8,128)(2,1)S(1)} %get-tuple-element.21.gtok_v, ...), custom_call_target="tpu_custom_call" | custom-call | tf_op jit(solution)/shard_map/pallas_call | solution.py:581
